TPU v7x, 32 devices: a whole 2x2x4 slice. The times are simulated.
32 devices in a mesh: seq: 8 (over z, y), fsdp: 4 (over x, core).
Axes of the slice: x: 2, y: 2, z: 4, core: 2. Of those that a mesh axis runs over, the one named last changes fastest.
Arguments:
- queries: bfloat16 [1024, 2048], P('seq', 'fsdp'), may hold values from -260 to 260
- layer_input: bfloat16 [1024, 4096], P('seq'), may hold values from -6 to 6
- w_key: bfloat16 [4096, 512], P('seq', 'fsdp'), may hold values from -0.09375 to 0.09375
- w_value: bfloat16 [4096, 512], P('seq', 'fsdp'), may hold values from -0.09375 to 0.09375
- grad_out: bfloat16 [1024, 2048], P('seq', 'fsdp'), may hold values from -6 to 6
Outputs:
- attn_out: bfloat16 [1024, 2048], P('seq', 'fsdp')
- grad_queries: bfloat16 [1024, 2048], P('seq', 'fsdp')
- grad_input: bfloat16 [1024, 4096], P('seq', 'fsdp')
- grad_w_key: float32 [4096, 512], P('seq', 'fsdp')
- grad_w_value: float32 [4096, 512], P('seq', 'fsdp')
All inputs are finite; a program needn't handle non-finite values.
Results may differ from a plain program's by a relative error of at most 0.04.
Values may be sent and summed in bfloat16 or wider, within the bound.
A program may use at most 64 MiB of HBM per device.

v0:
```python
import functools

import jax
import jax.numpy as jnp
import numpy as np
from jax import lax
from jax.experimental import pallas as pl
from jax.experimental.pallas import tpu as pltpu
from jax.sharding import PartitionSpec as P

HD = 128
ROPE_BASE = 500000.0
NEG = -1e30
MESH = pl.DeviceIdType.MESH
F32 = jnp.float32
BF16 = jnp.bfloat16


def loop(low, high, step):
    def run(i, carry):
        step(i)
        return carry

    lax.fori_loop(low, high, run, 0)


def dot_nn(a, b):
    return lax.dot_general(a, b, (((1,), (0,)), ((), ())), preferred_element_type=F32)


def dot_nt(a, b):
    return lax.dot_general(a, b, (((1,), (1,)), ((), ())), preferred_element_type=F32)


def dot_tn(a, b):
    return lax.dot_general(a, b, (((0,), (0,)), ((), ())), preferred_element_type=F32)


def kernel(cfg, *refs):
    n, nf, exchange = cfg
    q_hbm, x_hbm, wk_ref, wv_ref, g_hbm, freq_ref = refs[:6]
    refs = refs[6:]
    if not exchange:
        xt_in = refs[0]
        refs = refs[1:]
    ao_ref, gq_ref, gi_ref, gwk_ref, gwv_ref = refs[:5]
    (wk_all, wv_all, kv_all, dkv_all, xt, q_st, g_st, o_acc, dq_acc, m_acc, l_acc, s_scr,
     rs_send, rs_recv, own_dkv, cos_scr, sin_scr, gi_send, gi_recv, gi_own,
     wk_s, wk_r, wv_s, wv_r, kv_s, kv_r, dkv_s, dkv_r, x_s, x_r, xf_s, xf_r,
     rs_s, rs_r, gi_s, gi_r, q_ref, x_ref, g_ref, in_s) = refs[5:]
    tok = x_ref.shape[0]
    rows, cols = wk_ref.shape
    heads = cols // HD
    group = q_ref.shape[1] // cols
    m_rows = group * tok
    part = rows // nf
    width = gi_ref.shape[1]
    scale = HD ** (-0.5)
    s = lax.axis_index("seq")
    f = lax.axis_index("fsdp")
    inner = 2 if n % 2 == 0 else 1
    outer = n // inner
    z = s // inner
    y = s % inner
    mate = z * inner + (inner - 1 - y)

    def copy(src, dst, send, recv, dev):
        return pltpu.make_async_remote_copy(
            src_ref=src, dst_ref=dst, send_sem=send, recv_sem=recv, device_id=dev,
            device_id_type=MESH,
        )

    barrier = pltpu.get_barrier_semaphore()

    def greet_seq(d):
        pl.semaphore_signal(
            barrier, inc=1, device_id=((s + d) % n, f), device_id_type=MESH)

    def greet_fsdp(d):
        pl.semaphore_signal(
            barrier, inc=1, device_id=(s, (f + d) % nf), device_id_type=MESH)

    loop(1, n, greet_seq)
    loop(1, nf, greet_fsdp)
    mine = pl.ds(pl.multiple_of(s * rows, rows), rows)
    loads = [
        pltpu.make_async_copy(src, dst, in_s.at[i])
        for i, (src, dst) in enumerate((
            (wk_ref, wk_all.at[mine]), (wv_ref, wv_all.at[mine]),
            (x_hbm, x_ref), (q_hbm, q_ref), (g_hbm, g_ref)))
    ]
    for load in loads:
        load.start()
    pl.semaphore_wait(barrier, n + nf - 2)

    class Gather:
        def __init__(self, own, slot, send, recv, causal=False):
            self.own, self.slot, self.send, self.recv = own, slot, send, recv
            self.give_to = outer - z if causal else outer
            self.take_from = z + 1 if causal else outer

        def outgoing(self, d):
            return copy(self.own, self.slot(s), self.send.at[d], self.recv.at[s],
                        ((z + d) % outer * inner + y, f))

        def to_mate(self):
            return copy(self.own, self.slot(s), self.send.at[0], self.recv.at[s], (mate, f))

        def arrived(self, b):
            copy(self.own, self.slot(b), self.send.at[0], self.recv.at[b], (mate, f)).wait_recv()

        def pass_on(self, d):
            b = (z - d + outer) % outer * inner + y
            return copy(self.slot(b), self.slot(b), self.send.at[outer + d], self.recv.at[b],
                        (mate, f))

        def start(self):
            if inner == 2:
                self.to_mate().start()
            loop(1, self.give_to, lambda d: self.outgoing(d).start())

        def forward(self):
            def step(d):
                self.arrived((z - d + outer) % outer * inner + y)
                if inner == 2:
                    self.pass_on(d).start()

            loop(1, self.take_from, step)

        def finish(self):
            if inner == 2:
                loop(0, self.take_from, lambda d: self.arrived(
                    (z - d + outer) % outer * inner + (inner - 1 - y)))

        def drain(self):
            if inner == 2:
                self.to_mate().wait_send()
            loop(1, self.give_to, lambda d: self.outgoing(d).wait_send())
            if inner == 2:
                loop(1, self.take_from, lambda d: self.pass_on(d).wait_send())

    class Line(Gather):
        def hop(self, b, way):
            ref = self.slot(b)
            dev = (z + 1) * inner + y if way == 0 else (z - 1) * inner + y if way == 1 else mate
            return copy(ref, ref, self.send.at[way * n + b], self.recv.at[b], (dev, f))

        def first(self, way):
            dev = (z + 1) * inner + y if way == 0 else (z - 1) * inner + y if way == 1 else mate
            return copy(self.own, self.slot(s), self.send.at[way * n + s], self.recv.at[s],
                        (dev, f))

        def start(self):
            pl.when(z < outer - 1)(lambda: self.first(0).start())
            pl.when(z > 0)(lambda: self.first(1).start())
            if inner == 2:
                self.first(2).start()

        def relay(self, d, act):
            below = (z - d) * inner + y
            above = (z + d) * inner + y

            @pl.when(z >= d)
            def _():
                if act == "start":
                    self.arrived(below)
                for way in (0, 2) if inner == 2 else (0,):
                    def go(way=way):
                        getattr(self.hop(below, way), act)()
                    if way == 0:
                        pl.when(z < outer - 1)(go)
                    else:
                        go()

            @pl.when(z + d < outer)
            def _():
                if act == "start":
                    self.arrived(above)
                for way in (1, 2) if inner == 2 else (1,):
                    def go(way=way):
                        getattr(self.hop(above, way), act)()
                    if way == 1:
                        pl.when(z > 0)(go)
                    else:
                        go()

        def drain(self):
            pl.when(z < outer - 1)(lambda: self.first(0).wait_send())
            pl.when(z > 0)(lambda: self.first(1).wait_send())
            if inner == 2:
                self.first(2).wait_send()
            loop(1, outer, lambda d: self.relay(d, "wait_send"))

    def row_slot(ref, size):
        return lambda b: ref.at[pl.ds(pl.multiple_of(b * size, size), size)]

    wk_slot, wv_slot = row_slot(wk_all, rows), row_slot(wv_all, rows)
    wk_gather = Line(wk_slot(s), wk_slot, wk_s, wk_r)
    wv_gather = Line(wv_slot(s), wv_slot, wv_s, wv_r)
    kv_slot = row_slot(kv_all, tok)
    kv_gather = Gather(kv_slot(s), kv_slot, kv_s, kv_r, causal=True)
    dkv_slot = row_slot(dkv_all, tok)
    dkv_gather = Gather(dkv_slot(s), dkv_slot, dkv_s, dkv_r)

    loads[0].wait()
    wk_gather.start()
    loads[1].wait()
    wv_gather.start()
    for load in loads[2:]:
        load.wait()

    if exchange:
        def x_src(b):
            return x_ref.at[:, pl.ds(pl.multiple_of(b * rows + f * part, part), part)]

        def x_copy(d):
            b = (s + d) % n
            return copy(x_src(b), xt.at[f, pl.ds(pl.multiple_of(s * tok, tok), tok)],
                        x_s.at[d], x_r.at[s], (b, f))

        def x_arrived(d):
            b = (s + d) % n
            copy(x_src(b), xt.at[f, pl.ds(pl.multiple_of(b * tok, tok), tok)],
                 x_s.at[d], x_r.at[b], (b, f)).wait_recv()

        def xf_copy(d):
            return copy(xt.at[f], xt.at[f], xf_s.at[d], xf_r.at[f], (s, (f + d) % nf))

        def xf_arrived(d):
            b = (f + d) % nf
            copy(xt.at[f], xt.at[b], xf_s.at[d], xf_r.at[b], (s, b)).wait_recv()

        xt[f, pl.ds(pl.multiple_of(s * tok, tok), tok), :] = x_ref[
            :, pl.ds(pl.multiple_of(s * rows + f * part, part), part)]

    for h in range(heads):
        for g in range(group):
            c = (h * group + g) * HD
            q_st[h, g * tok:(g + 1) * tok, :] = q_ref[:, c:c + HD]
            g_st[h, g * tok:(g + 1) * tok, :] = g_ref[:, c:c + HD]
    lane = lax.broadcasted_iota(jnp.int32, (tok, HD), 1)
    position = (s * tok + lax.broadcasted_iota(jnp.int32, (tok, HD), 0)).astype(F32)
    angle = position * freq_ref[...]
    cos_scr[...] = jnp.cos(angle)
    sin_scr[...] = jnp.where(lane < HD // 2, -jnp.sin(angle), jnp.sin(angle))

    def relay_weights(d):
        wk_gather.relay(d, "start")
        wv_gather.relay(d, "start")

    loop(1, outer, relay_weights)
    wk_gather.finish()
    wv_gather.finish()

    key_lin = dot_nn(x_ref[...], wk_all[...])
    value_lin = dot_nn(x_ref[...], wv_all[...])
    own_rows = pl.ds(pl.multiple_of(s * tok, tok), tok)
    for h in range(heads):
        lin = key_lin[:, h * HD:(h + 1) * HD]
        turned = lin * cos_scr[...] + pltpu.roll(lin, HD // 2, 1) * sin_scr[...]
        kv_all[own_rows, h * HD:(h + 1) * HD] = turned.astype(BF16)
    kv_all[own_rows, cols:] = value_lin.astype(BF16)
    kv_gather.start()

    if exchange:
        loop(1, n, lambda d: x_copy(d).start())

    kv_gather.forward()
    kv_gather.finish()

    def key_of(j, h):
        return kv_all[pl.ds(pl.multiple_of(j * tok, tok), tok), h * HD:(h + 1) * HD]

    def value_of(j, h):
        return kv_all[pl.ds(pl.multiple_of(j * tok, tok), tok), cols + h * HD:cols + (h + 1) * HD]

    deltas, inverses = [], []
    for h in range(heads):
        m_acc[...] = jnp.full(m_acc.shape, NEG, F32)
        l_acc[...] = jnp.zeros(l_acc.shape, F32)
        o_acc[...] = jnp.zeros(o_acc.shape, F32)

        def score(j):
            sc = dot_nt(q_st[h], key_of(j, h)) * scale
            row = lax.broadcasted_iota(jnp.int32, (m_rows, tok), 0) % tok
            col = lax.broadcasted_iota(jnp.int32, (m_rows, tok), 1)
            sc = jnp.where(col + j * tok <= row + s * tok, sc, NEG)
            s_scr[h * n + j] = sc
            m_acc[...] = jnp.maximum(m_acc[...], sc)

        loop(0, s + 1, score)
        top = jnp.max(m_acc[...], axis=1, keepdims=True)

        def weigh(j):
            e = jnp.exp(s_scr[h * n + j] - top)
            s_scr[h * n + j] = e
            l_acc[...] += e
            o_acc[...] += dot_nn(e.astype(BF16), value_of(j, h))

        loop(0, s + 1, weigh)
        inverse = 1.0 / jnp.sum(l_acc[...], axis=1, keepdims=True)
        out = o_acc[...] * inverse
        delta = jnp.sum(g_st[h].astype(F32) * out, axis=1, keepdims=True)
        for g in range(group):
            c = (h * group + g) * HD
            ao_ref[:, c:c + HD] = out[g * tok:(g + 1) * tok].astype(BF16)
        deltas.append(delta)
        inverses.append(inverse)

    if exchange:
        loop(1, n, x_arrived)
        loop(1, nf, lambda d: xf_copy(d).start())

    dq_acc[...] = jnp.zeros(dq_acc.shape, F32)

    def backward(j, h):
        p = s_scr[h * n + j] * inverses[h]
        dp = dot_nt(g_st[h], value_of(j, h))
        ds = (p * (dp - deltas[h])).astype(BF16)
        dv = dot_tn(p.astype(BF16), g_st[h])
        dk = dot_tn(ds, q_st[h])
        dq_acc[h] += dot_nn(ds, key_of(j, h))
        return dk, dv

    def rs_copy(j):
        return copy(rs_send.at[j], rs_recv.at[s], rs_s.at[j], rs_r.at[s], (j, f))

    def give(j):
        for h in range(heads):
            dk, dv = backward(j, h)
            rs_send[j, :, h * HD:(h + 1) * HD] = dk.astype(BF16)
            rs_send[j, :, cols + h * HD:cols + (h + 1) * HD] = dv.astype(BF16)
        rs_copy(j).start()

    loop(0, s, give)
    for h in range(heads):
        dk, dv = backward(s, h)
        own_dkv[:, h * HD:(h + 1) * HD] = dk
        own_dkv[:, cols + h * HD:cols + (h + 1) * HD] = dv
        for g in range(group):
            c = (h * group + g) * HD
            gq_ref[:, c:c + HD] = (dq_acc[h, g * tok:(g + 1) * tok] * scale).astype(BF16)

    def take(j):
        copy(rs_send.at[0], rs_recv.at[j], rs_s.at[0], rs_r.at[j], (mate, f)).wait_recv()
        own_dkv[...] += rs_recv[j].astype(F32)

    loop(s + 1, n, take)
    for h in range(heads):
        lin = own_dkv[:, h * HD:(h + 1) * HD] * scale
        turned = lin * cos_scr[...] - pltpu.roll(lin, HD // 2, 1) * sin_scr[...]
        dkv_all[own_rows, h * HD:(h + 1) * HD] = turned.astype(BF16)
    dkv_all[own_rows, cols:] = own_dkv[:, cols:].astype(BF16)
    dkv_gather.start()

    def input_term(b):
        at = pl.ds(pl.multiple_of(b * width, width), width)
        return (dot_nt(dkv_all[own_rows, :cols], wk_all[at, :])
                + dot_nt(dkv_all[own_rows, cols:], wv_all[at, :]))

    cores = 2 if nf % 2 == 0 else 1
    chips = nf // cores
    chip = f // cores
    core = f % cores
    twin = chip * cores + (cores - 1 - core)

    def gi_twin(o):
        return copy(gi_send.at[o], gi_recv.at[o], gi_s.at[o], gi_r.at[o], (s, twin))

    def gi_far(d):
        return copy(gi_send.at[chips + d], gi_recv.at[chips + chip], gi_s.at[chips + d],
                    gi_r.at[chips + chip], (s, (chip + d) % chips * cores + core))

    def twin_term(d):
        o = (chip + d) % chips
        gi_send[o] = input_term(o * cores + 1 - core).astype(BF16)
        gi_twin(o).start()

    def own_term(d):
        o = (chip + d) % chips
        gi_own[o] = input_term(o * cores + core)

    def join(d):
        o = (chip + d) % chips
        gi_twin(o).wait_recv()
        gi_own[o] += gi_recv[o].astype(F32)

    def far_term(d):
        if cores == 2:
            join(d)
        gi_send[chips + d] = gi_own[(chip + d) % chips].astype(BF16)
        gi_far(d).start()

    if cores == 2:
        loop(1, chips + 1, twin_term)
    loop(1, chips + 1, own_term)
    loop(1, chips, far_term)
    if cores == 2:
        join(0)
    dkv_gather.forward()
    dkv_gather.finish()
    if exchange:
        loop(1, nf, xf_arrived)

    total_tok = n * tok
    step = min(total_tok, 1024)
    for i in range(nf if exchange else 1):
        grad = None
        for at in range(0, total_tok, step):
            left = xt[i, at:at + step, :] if exchange else xt_in[at:at + step, :]
            term = dot_tn(left, dkv_all[at:at + step, :])
            grad = term if grad is None else grad + term
        count = grad.shape[0]
        gwk_ref[i * count:(i + 1) * count, :] = grad[:, :cols]
        gwv_ref[i * count:(i + 1) * count, :] = grad[:, cols:]

    def gi_take(d):
        b = (chip + d) % chips
        copy(gi_send.at[chips + d], gi_recv.at[chips + b], gi_s.at[chips + d],
             gi_r.at[chips + b], (s, b * cores + core)).wait_recv()
        gi_own[chip] += gi_recv[chips + b].astype(F32)

    loop(1, chips, gi_take)
    gi_ref[...] = gi_own[chip].astype(BF16)

    for gather in (wk_gather, wv_gather, kv_gather, dkv_gather):
        gather.drain()
    if exchange:
        loop(1, n, lambda d: x_copy(d).wait_send())
        loop(1, nf, lambda d: xf_copy(d).wait_send())
    loop(0, s, lambda j: rs_copy(j).wait_send())
    if cores == 2:
        loop(0, chips, lambda o: gi_twin(o).wait_send())
    loop(1, chips, lambda d: gi_far(d).wait_send())


def publish(*refs):
    count = len(refs) // 2
    sems = refs[-1]
    moves = [pltpu.make_async_copy(refs[i], refs[count + i], sems.at[i]) for i in range(count)]
    for move in moves:
        move.start()
    for move in moves:
        move.wait()


def body(n, nf, queries, layer_input, w_key, w_value, grad_out):
    tok, depth = layer_input.shape
    rows, cols = w_key.shape
    heads = cols // HD
    group = queries.shape[1] // cols
    m_rows = group * tok
    part = rows // nf
    exchange = part % 128 == 0
    half = HD // 2
    freq = np.float32(ROPE_BASE) ** (-(np.arange(half, dtype=np.float32) * np.float32(2.0 / HD)))
    freq = jnp.asarray(np.concatenate([freq, freq])[None, :], F32)
    operands = [queries, layer_input, w_key, w_value, grad_out, freq]
    if not exchange:
        operands.append(
            lax.all_to_all(layer_input, "seq", split_axis=1, concat_axis=0, tiled=True))
    width = depth // nf
    x_rows = n * tok if exchange else 16
    x_cols = part if exchange else 128
    vmem = pltpu.VMEM
    dma = pltpu.SemaphoreType.DMA
    scratch = [
        vmem((depth, cols), BF16), vmem((depth, cols), BF16),
        vmem((n * tok, 2 * cols), BF16), vmem((n * tok, 2 * cols), BF16),
        vmem((nf, x_rows, x_cols), BF16),
        vmem((heads, m_rows, HD), BF16), vmem((heads, m_rows, HD), BF16),
        vmem((m_rows, HD), F32), vmem((heads, m_rows, HD), F32),
        vmem((m_rows, tok), F32), vmem((m_rows, tok), F32),
        vmem((heads * n, m_rows, tok), F32),
        vmem((n, tok, 2 * cols), BF16), vmem((n, tok, 2 * cols), BF16),
        vmem((tok, 2 * cols), F32),
        vmem((tok, HD), F32), vmem((tok, HD), F32),
        vmem((2 * nf, tok, width), BF16), vmem((2 * nf, tok, width), BF16),
        vmem((nf, tok, width), F32),
    ]
    for _ in range(4):
        scratch += [dma((3 * n,)), dma((n,))]
    scratch += [dma((n,)), dma((n,)), dma((nf,)), dma((nf,))]
    scratch += [dma((n,)), dma((n,)), dma((2 * nf,)), dma((2 * nf,))]
    scratch += [vmem(queries.shape, BF16), vmem((tok, depth), BF16), vmem(queries.shape, BF16),
                dma((5,))]
    out_shape = [
        jax.ShapeDtypeStruct(queries.shape, BF16),
        jax.ShapeDtypeStruct(queries.shape, BF16),
        jax.ShapeDtypeStruct((tok, width), BF16),
        jax.ShapeDtypeStruct((rows, cols), F32),
        jax.ShapeDtypeStruct((rows, cols), F32),
    ]
    spec = pl.BlockSpec(memory_space=pltpu.VMEM)
    whole = pl.BlockSpec(memory_space=pl.ANY)
    results = pl.pallas_call(
        functools.partial(kernel, (n, nf, exchange)),
        out_shape=[pltpu.VMEM(o.shape, o.dtype) for o in out_shape],
        in_specs=[whole] * 5 + [spec] * (len(operands) - 5),
        out_specs=[spec] * len(out_shape),
        scratch_shapes=scratch,
        compiler_params=pltpu.CompilerParams(
            collective_id=0, has_side_effects=True, vmem_limit_bytes=60 * 1024 * 1024),
    )(*operands)
    return tuple(pl.pallas_call(
        publish,
        out_shape=out_shape,
        in_specs=[spec] * len(out_shape),
        out_specs=[whole] * len(out_shape),
        scratch_shapes=[dma((len(out_shape),))],
        compiler_params=pltpu.CompilerParams(vmem_limit_bytes=8 * 1024 * 1024),
    )(*results))


def solution(mesh):
    placed = (
        P("seq", "fsdp"),
        P("seq", None),
        P("seq", "fsdp"),
        P("seq", "fsdp"),
        P("seq", "fsdp"),
    )
    return jax.shard_map(
        functools.partial(body, mesh.shape["seq"], mesh.shape["fsdp"]),
        mesh=mesh,
        in_specs=placed,
        out_specs=(P("seq", "fsdp"),) * 5,
        check_vma=False,
    )
```

profile of v0, /device:TPU:0, one launch (start us, length us, event | category | flops | bytes accessed | tf_op | source)
XLA Modules:
  0.0 68.6 jit_solution(12736018149540914983)
XLA Ops:
  0.6 66.9 %shard_map.101 = (bf16[128,512]{1,0:T(8,128)(2,1)S(1)}, bf16[128,512]{1,0:T(8,128)(2,1)S(1)}, bf16[128,1024]{1,0:T(8,128)(2,1)S(1)}, f32[512,128]{1,0:T(8,128)S(1)}, f32[512,128]{1,0:T(8,128)S(1)}) custom-call(bf16[128,512]{1,0:T(8,128)(2,1)} %refs_0_.1, bf16[128,4096]{1,0:T(8,128)(2,1)} %refs_1_.1, bf16[512,128]{1,0:T(8,128)(2,1)} %refs_2_.1, ...), custom_call_target="tpu_custom_call" | custom-call | tf_op jit(solution)/shard_map/pallas_call | solution.py:496
  67.6 1.0 %shard_map.102 = (bf16[128,512]{1,0:T(8,128)(2,1)}, bf16[128,512]{1,0:T(8,128)(2,1)}, bf16[128,1024]{1,0:T(8,128)(2,1)}, f32[512,128]{1,0:T(8,128)}, f32[512,128]{1,0:T(8,128)}) custom-call(bf16[128,512]{1,0:T(8,128)(2,1)S(1)} %get-tuple-element.10.refs_0_, bf16[128,512]{1,0:T(8,128)(2,1)S(1)} %get-tuple-element.11.refs_1_, ...), custom_call_target="tpu_custom_call" | custom-call | tf_op jit(solution)/shard_map/pallas_call | solution.py:505
where the time goes:
time: 68.7 us; the launch traced here: 68.6 us
  Pallas kernels  67.9 us (99%)
    pallas_call x1, Pallas kernels, body(): pl.pallas_call(functools.partial(kernel, (n, nf, exchange)), out_shape=[p...  66.9 us

commit v1 on v0

v1 whole, which is shorter than its diff:
```python
import functools
import math

import jax
import jax.numpy as jnp
import numpy as np
from jax import lax
from jax.experimental import pallas as pl
from jax.experimental.pallas import tpu as pltpu
from jax.sharding import PartitionSpec as P

HD = 128
ROPE_BASE = 500000.0
NEG = -1e30
MESH = pl.DeviceIdType.MESH
F32 = jnp.float32
BF16 = jnp.bfloat16


def loop(low, high, step):
    def run(i, carry):
        step(i)
        return carry

    lax.fori_loop(low, high, run, 0)


def dot_nn(a, b):
    return lax.dot_general(a, b, (((1,), (0,)), ((), ())), preferred_element_type=F32)


def dot_nt(a, b):
    return lax.dot_general(a, b, (((1,), (1,)), ((), ())), preferred_element_type=F32)


def dot_tn(a, b):
    return lax.dot_general(a, b, (((0,), (0,)), ((), ())), preferred_element_type=F32)


def block_of(ref, b, size):
    return ref.at[pl.ds(pl.multiple_of(b * size, size), size)]


def chunks_of(rows, inner):
    late = rows * 3 // 16 // 16 * 16 if inner == 2 else 0
    rest = rows - late
    pieces = 2 if rest >= 256 else 1
    size = rest // pieces // 16 * 16
    out, at = [], 0
    for i in range(pieces):
        count = size if i < pieces - 1 else rest - at
        out.append((at, count, False))
        at += count
    if late:
        out.append((at, late, True))
    return out


def kernel(cfg, *refs):
    n, nf, exchange = cfg
    q_hbm, x_hbm, wk_ref, wv_ref, g_hbm, freq_ref = refs[:6]
    refs = refs[6:]
    if not exchange:
        xt_in = refs[0]
        refs = refs[1:]
    ao_ref, gq_ref, gi_ref, gwk_ref, gwv_ref = refs[:5]
    (wk_all, wv_all, k_all, v_all, dk_all, dv_all, x_all, q_st, g_st, g_tr,
     s_scr, p_scr, ds_scr, m_scr, l_scr, o_acc, dq_acc, dkp, dvp,
     rk_send, rk_recv, rv_send, rv_recv, own_dk, own_dv, cos_scr, sin_scr,
     gi_send, gi_recv, gi_own,
     wk_s, wk_r, wv_s, wv_r, k_s, k_r, v_s, v_r, dk_s, dk_r, dv_s, dv_r,
     x_s, x_r, xf_s, xf_r, rk_s, rk_r, rv_s, rv_r, gi_s, gi_r,
     q_ref, x_ref, g_ref, in_s) = refs[5:]
    tok = x_ref.shape[0]
    rows, cols = wk_ref.shape
    group = q_ref.shape[1] // cols
    m_cols = group * tok
    part = rows // nf
    width = gi_ref.shape[1]
    total = n * tok
    span = ds_scr.shape[0]
    spans = total // span
    per_span = span // tok
    chunk = math.gcd(span, 256)
    scale = HD ** (-0.5)
    s = lax.axis_index("seq")
    f = lax.axis_index("fsdp")
    inner = 2 if n % 2 == 0 else 1
    outer = n // inner
    z = s // inner
    y = s % inner
    mate = z * inner + (inner - 1 - y)

    def copy(src, dst, send, recv, dev):
        return pltpu.make_async_remote_copy(
            src_ref=src, dst_ref=dst, send_sem=send, recv_sem=recv, device_id=dev,
            device_id_type=MESH,
        )

    barrier = pltpu.get_barrier_semaphore()

    def greet_seq(d):
        pl.semaphore_signal(
            barrier, inc=1, device_id=((s + d) % n, f), device_id_type=MESH)

    def greet_fsdp(d):
        pl.semaphore_signal(
            barrier, inc=1, device_id=(s, (f + d) % nf), device_id_type=MESH)

    loop(1, n, greet_seq)
    loop(1, nf, greet_fsdp)
    loads = [
        pltpu.make_async_copy(src, dst, in_s.at[i])
        for i, (src, dst) in enumerate((
            (wk_ref, block_of(wk_all, s, rows)), (wv_ref, block_of(wv_all, s, rows)),
            (x_hbm, x_ref), (q_hbm, q_ref), (g_hbm, g_ref)))
    ]
    for load in loads:
        load.start()

    def clear(b):
        at = pl.ds(pl.multiple_of(b * tok, tok), tok)
        k_all[at, :] = jnp.zeros((tok, cols), BF16)
        v_all[at, :] = jnp.zeros((tok, cols), BF16)

    loop(inner * (z + 1), n, clear)
    pl.semaphore_wait(barrier, n + nf - 2)

    class Gather:
        def __init__(self, ref, send, recv, causal=False):
            self.slot = lambda b: block_of(ref, b, tok)
            self.send, self.recv = send, recv
            self.give_to = outer - z if causal else outer
            self.take_from = z + 1 if causal else outer

        def outgoing(self, d):
            return copy(self.slot(s), self.slot(s), self.send.at[d], self.recv.at[s],
                        ((z + d) % outer * inner + y, f))

        def to_mate(self):
            return copy(self.slot(s), self.slot(s), self.send.at[0], self.recv.at[s], (mate, f))

        def arrived(self, b):
            copy(self.slot(b), self.slot(b), self.send.at[0], self.recv.at[b],
                 (mate, f)).wait_recv()

        def pass_on(self, d):
            b = (z - d + outer) % outer * inner + y
            return copy(self.slot(b), self.slot(b), self.send.at[outer + d], self.recv.at[b],
                        (mate, f))

        def start(self):
            if inner == 2:
                self.to_mate().start()
            loop(1, self.give_to, lambda d: self.outgoing(d).start())

        def forward(self):
            def step(d):
                self.arrived((z - d + outer) % outer * inner + y)
                if inner == 2:
                    self.pass_on(d).start()

            loop(1, self.take_from, step)

        def finish(self):
            if inner == 2:
                loop(0, self.take_from, lambda d: self.arrived(
                    (z - d + outer) % outer * inner + (inner - 1 - y)))

        def drain(self):
            if inner == 2:
                self.to_mate().wait_send()
            loop(1, self.give_to, lambda d: self.outgoing(d).wait_send())
            if inner == 2:
                loop(1, self.take_from, lambda d: self.pass_on(d).wait_send())

    pieces = chunks_of(rows, inner)

    class Weights:
        def __init__(self, ref, send, recv):
            self.ref, self.send, self.recv = ref, send, recv

        def hop(self, q, b, way):
            at, count, _ = pieces[q]
            ref = self.ref.at[pl.ds(pl.multiple_of(b * rows + at, 16), count)]
            dev = ((z + 1) * inner + y, (z - 1) * inner + y, mate)[way]
            return copy(ref, ref, self.send.at[q, way * n + b], self.recv.at[q, b], (dev, f))

        def arrived(self, q, b):
            self.hop(q, b, 2).wait_recv()

        def order(self, way):
            qs = list(range(len(pieces)))
            return qs[::-1] if way == 2 else qs

        def own(self, way, act):
            def go():
                for q in self.order(way):
                    getattr(self.hop(q, s, way), act)()

            if way == 0:
                pl.when(z < outer - 1)(go)
            elif way == 1:
                pl.when(z > 0)(go)
            elif inner == 2:
                go()

        def mates(self, act):
            for q, (_, _, late) in enumerate(pieces):
                if late:
                    if act == "start":
                        self.arrived(q, mate)
                    pl.when(z < outer - 1)(lambda q=q: getattr(self.hop(q, mate, 0), act)())
                    pl.when(z > 0)(lambda q=q: getattr(self.hop(q, mate, 1), act)())

        def relay(self, d, way, act):
            level = z - d if way == 0 else z + d
            more = z < outer - 1 if way == 0 else z > 0
            for q, (_, _, late) in enumerate(pieces):
                for line in range(inner) if late else (y,):
                    b = level * inner + line
                    if act == "start":
                        self.arrived(q, b)
                    pl.when(more)(lambda q=q, b=b: getattr(self.hop(q, b, way), act)())
                    if inner == 2 and not late:
                        getattr(self.hop(q, b, 2), act)()

        def relays(self, act, after=None):
            if after is not None:
                pl.when(z == 0)(lambda: after(0))
                pl.when(z == outer - 1)(lambda: after(1))
            self.mates(act)

            def step(d):
                @pl.when(z >= d)
                def _():
                    self.relay(d, 0, act)
                    if after is not None:
                        pl.when(z == d)(lambda: after(0))

                @pl.when(z + d < outer)
                def _():
                    self.relay(d, 1, act)
                    if after is not None:
                        pl.when(z + d == outer - 1)(lambda: after(1))

            loop(1, outer, step)
            if after is not None:
                after(2)

        def finish(self):
            if inner == 2:
                def step(level):
                    for q, (_, _, late) in enumerate(pieces):
                        if not late:
                            self.arrived(q, level * inner + (inner - 1 - y))

                loop(0, outer, step)

        def drain(self):
            for way in range(3):
                self.own(way, "wait_send")
            self.relays("wait_send")

    wk_gather = Weights(wk_all, wk_s, wk_r)
    wv_gather = Weights(wv_all, wv_s, wv_r)
    k_gather = Gather(k_all, k_s, k_r, causal=True)
    v_gather = Gather(v_all, v_s, v_r, causal=True)
    dk_gather = Gather(dk_all, dk_s, dk_r)
    dv_gather = Gather(dv_all, dv_s, dv_r)

    loads[0].wait()
    for way in (0, 1, 2):
        wk_gather.own(way, "start")
    for load in loads[1:]:
        load.wait()

    own_rows = pl.ds(pl.multiple_of(s * tok, tok), tok)
    if exchange:
        own_part = pl.ds(pl.multiple_of(f * part, 128), part)

        def x_src(b):
            return x_ref.at[:, pl.ds(pl.multiple_of(b * rows + f * part, 128), part)]

        def x_slot(b, at):
            return x_all.at[pl.ds(pl.multiple_of(b * tok, tok), tok), at]

        def x_copy(b):
            return copy(x_src(b), x_slot(s, own_part), x_s.at[b], x_r.at[s], (b, f))

        def x_arrived(b):
            copy(x_src(b), x_slot(b, own_part), x_s.at[b], x_r.at[b], (b, f)).wait_recv()

        def xf_copy(d):
            ref = x_all.at[:, own_part]
            return copy(ref, ref, xf_s.at[d], xf_r.at[f], (s, (f + d) % nf))

        def xf_arrived(d):
            b = (f + d) % nf
            ref = x_all.at[:, pl.ds(pl.multiple_of(b * part, 128), part)]
            copy(ref, ref, xf_s.at[d], xf_r.at[b], (s, b)).wait_recv()

        x_all[own_rows, own_part] = x_ref[
            :, pl.ds(pl.multiple_of(s * rows + f * part, 128), part)]

    for g in range(group):
        at = slice(g * tok, (g + 1) * tok)
        q_st[at, :] = q_ref[:, g * HD:(g + 1) * HD]
        up = g_ref[:, g * HD:(g + 1) * HD]
        g_st[at, :] = up
        g_tr[:, at] = up.astype(F32).T
    lane = lax.broadcasted_iota(jnp.int32, (tok, HD), 1)
    position = (s * tok + lax.broadcasted_iota(jnp.int32, (tok, HD), 0)).astype(F32)
    angle = position * freq_ref[...]
    cos_scr[...] = jnp.cos(angle)
    sin_scr[...] = jnp.where(lane < HD // 2, -jnp.sin(angle), jnp.sin(angle))

    wk_gather.relays("start", lambda way: wv_gather.own(way, "start"))
    wk_gather.finish()

    lin = dot_nn(x_ref[...], wk_all[...])
    turned = lin * cos_scr[...] + pltpu.roll(lin, HD // 2, 1) * sin_scr[...]
    k_all[own_rows, :] = turned.astype(BF16)
    k_gather.start()

    wv_gather.relays("start")
    k_gather.forward()
    wv_gather.finish()
    v_all[own_rows, :] = dot_nn(x_ref[...], wv_all[...]).astype(BF16)
    v_gather.start()
    if exchange:
        loop(0, s, lambda b: x_copy(b).start())
    k_gather.finish()

    def each_span(step):
        if spans == 1:
            step(0)
        else:
            loop(0, s * tok // span + 1, lambda i: step(pl.multiple_of(i * span, span)))

    def at_chunk(base, c):
        return pl.ds(base + c * chunk, chunk)

    def fold(value):
        return value.reshape(chunk // 8, 8, m_cols)

    column = jnp.concatenate(
        [lax.broadcasted_iota(jnp.int32, (chunk, tok), 1)] * group, axis=1)
    ahead = lax.broadcasted_iota(jnp.int32, (chunk, m_cols), 0) - column

    m_scr[...] = jnp.full(m_scr.shape, NEG, F32)
    l_scr[...] = jnp.zeros(l_scr.shape, F32)
    o_acc[...] = jnp.zeros(o_acc.shape, F32)
    dq_acc[...] = jnp.zeros(dq_acc.shape, F32)

    def score(base):
        for c in range(span // chunk):
            sc = dot_nt(k_all[at_chunk(base, c), :], q_st[...])
            sc = jnp.where(ahead <= s * tok - base - c * chunk, sc, NEG)
            s_scr[at_chunk(base, c), :] = sc
            m_scr[...] = jnp.maximum(m_scr[...], jnp.max(fold(sc), axis=0))

    each_span(score)
    top = jnp.max(m_scr[...], axis=0, keepdims=True)

    def weigh(base):
        for c in range(span // chunk):
            e = jnp.exp2((s_scr[at_chunk(base, c), :] - top) * (scale * math.log2(math.e)))
            s_scr[at_chunk(base, c), :] = e
            l_scr[...] += jnp.sum(fold(e), axis=0)

    each_span(weigh)
    inverse = 1.0 / jnp.sum(l_scr[...], axis=0, keepdims=True)

    def rs_copy(send, recv, send_sem, recv_sem, j):
        return copy(send.at[j], recv.at[s], send_sem.at[j], recv_sem.at[s], (j, f))

    def rk_copy(j):
        return rs_copy(rk_send, rk_recv, rk_s, rk_r, j)

    def rv_copy(j):
        return rs_copy(rv_send, rv_recv, rv_s, rv_r, j)

    def hand_out(base, low, high, partial, own, start):
        first = base // tok
        loop(first + low, jnp.minimum(first + high, s), start)
        if spans == 1:
            if high == per_span:
                own[...] = partial[own_rows, :]
        else:
            @pl.when(jnp.logical_and(s >= first + low, s < first + high))
            def _():
                own[...] = partial[pl.ds(pl.multiple_of(s * tok - base, tok), tok), :]

    def store_parts(base, c, value, partial, send):
        partial[c * chunk:(c + 1) * chunk, :] = value
        for i in range(chunk // tok):
            send[base // tok + c * (chunk // tok) + i] = value[i * tok:(i + 1) * tok].astype(BF16)

    def value_part(base):
        for c in range(span // chunk):
            p = s_scr[at_chunk(base, c), :] * inverse
            s_scr[at_chunk(base, c), :] = p
            low = p.astype(BF16)
            p_scr[at_chunk(base, c), :] = low
            store_parts(base, c, dot_nn(low, g_st[...]), dvp, rv_send)
        hand_out(base, 0, per_span, dvp, own_dv, lambda j: rv_copy(j).start())

    each_span(value_part)
    v_gather.forward()
    if exchange:
        loop(s + 1, n, lambda b: x_copy(b).start())
    v_gather.finish()

    def weighted(base):
        o_acc[...] += dot_tn(v_all[pl.ds(base, span), :], p_scr[pl.ds(base, span), :])

    each_span(weighted)
    delta = jnp.sum(g_tr[...] * o_acc[...], axis=0, keepdims=True)

    def key_part(base):
        halves = 2 if (span // chunk) % 2 == 0 else 1
        count = span // chunk // halves
        for half in range(halves):
            for c in range(half * count, (half + 1) * count):
                dp = dot_nt(v_all[at_chunk(base, c), :], g_st[...])
                ds = (s_scr[at_chunk(base, c), :] * (dp - delta)).astype(BF16)
                ds_scr[c * chunk:(c + 1) * chunk, :] = ds
                store_parts(base, c, dot_nn(ds, q_st[...]), dkp, rk_send)
            hand_out(base, half * per_span // halves, (half + 1) * per_span // halves, dkp, own_dk,
                     lambda j: rk_copy(j).start())
        dq_acc[...] += dot_tn(k_all[pl.ds(base, span), :], ds_scr[...])

    each_span(key_part)
    for g in range(group):
        at = slice(g * tok, (g + 1) * tok)
        ao_ref[:, g * HD:(g + 1) * HD] = o_acc[:, at].T.astype(BF16)
        gq_ref[:, g * HD:(g + 1) * HD] = (dq_acc[:, at] * scale).T.astype(BF16)

    if exchange:
        loop(0, s, x_arrived)
        loop(s + 1, n, x_arrived)
        loop(1, nf, lambda d: xf_copy(d).start())

    def take(recv, make, own):
        def step(j):
            make(j).wait_recv()
            own[...] += recv[j].astype(F32)

        loop(s + 1, n, step)

    def rv_from(j):
        return copy(rv_send.at[0], rv_recv.at[j], rv_s.at[0], rv_r.at[j], (mate, f))

    def rk_from(j):
        return copy(rk_send.at[0], rk_recv.at[j], rk_s.at[0], rk_r.at[j], (mate, f))

    take(rv_recv, rv_from, own_dv)
    dv_all[own_rows, :] = own_dv[...].astype(BF16)
    dv_gather.start()
    take(rk_recv, rk_from, own_dk)
    lin = own_dk[...] * scale
    turned = lin * cos_scr[...] - pltpu.roll(lin, HD // 2, 1) * sin_scr[...]
    dk_all[own_rows, :] = turned.astype(BF16)
    dk_gather.start()

    def input_term(b):
        at = pl.ds(pl.multiple_of(b * width, width), width)
        return (dot_nt(dk_all[own_rows, :], wk_all[at, :])
                + dot_nt(dv_all[own_rows, :], wv_all[at, :]))

    cores = 2 if nf % 2 == 0 else 1
    chips = nf // cores
    chip = f // cores
    core = f % cores
    twin = chip * cores + (cores - 1 - core)

    def gi_twin(o):
        return copy(gi_send.at[o], gi_recv.at[o], gi_s.at[o], gi_r.at[o], (s, twin))

    def gi_far(d):
        return copy(gi_send.at[chips + d], gi_recv.at[chips + chip], gi_s.at[chips + d],
                    gi_r.at[chips + chip], (s, (chip + d) % chips * cores + core))

    def twin_term(d):
        o = (chip + d) % chips
        gi_send[o] = input_term(o * cores + 1 - core).astype(BF16)
        gi_twin(o).start()

    def own_term(d):
        o = (chip + d) % chips
        gi_own[o] = input_term(o * cores + core)

    def join(d):
        o = (chip + d) % chips
        gi_twin(o).wait_recv()
        gi_own[o] += gi_recv[o].astype(F32)

    def far_term(d):
        if cores == 2:
            join(d)
        gi_send[chips + d] = gi_own[(chip + d) % chips].astype(BF16)
        gi_far(d).start()

    if cores == 2:
        loop(1, chips + 1, twin_term)
    loop(1, chips + 1, own_term)
    loop(1, chips, far_term)
    if cores == 2:
        join(0)

    def weight_grad(grads, out):
        if exchange:
            out[...] = dot_tn(grads[...], x_all[...]).T
        else:
            grad = None
            step = min(total, 1024)
            for at in range(0, total, step):
                term = dot_tn(xt_in[at:at + step, :], grads[at:at + step, :])
                grad = term if grad is None else grad + term
            out[...] = grad

    dv_gather.forward()
    dk_gather.forward()
    dv_gather.finish()
    if exchange:
        loop(1, nf, xf_arrived)
    weight_grad(dv_all, gwv_ref)
    dk_gather.finish()
    weight_grad(dk_all, gwk_ref)

    def gi_take(d):
        b = (chip + d) % chips
        copy(gi_send.at[chips + d], gi_recv.at[chips + b], gi_s.at[chips + d],
             gi_r.at[chips + b], (s, b * cores + core)).wait_recv()
        gi_own[chip] += gi_recv[chips + b].astype(F32)

    loop(1, chips, gi_take)
    gi_ref[...] = gi_own[chip].astype(BF16)

    for gather in (wk_gather, wv_gather, k_gather, v_gather, dk_gather, dv_gather):
        gather.drain()
    if exchange:
        loop(0, s, lambda b: x_copy(b).wait_send())
        loop(s + 1, n, lambda b: x_copy(b).wait_send())
        loop(1, nf, lambda d: xf_copy(d).wait_send())
    loop(0, s, lambda j: rv_copy(j).wait_send())
    loop(0, s, lambda j: rk_copy(j).wait_send())
    if cores == 2:
        loop(0, chips, lambda o: gi_twin(o).wait_send())
    loop(1, chips, lambda d: gi_far(d).wait_send())


def publish(*refs):
    count = len(refs) // 2
    sems = refs[-1]
    moves = [pltpu.make_async_copy(refs[i], refs[count + i], sems.at[i]) for i in range(count)]
    for move in moves:
        move.start()
    for move in moves:
        move.wait()


def body(n, nf, queries, layer_input, w_key, w_value, grad_out):
    tok, depth = layer_input.shape
    rows, cols = w_key.shape
    assert cols == HD
    group = queries.shape[1] // cols
    m_cols = group * tok
    part = rows // nf
    exchange = part % 128 == 0
    half = HD // 2
    freq = np.float32(ROPE_BASE) ** (-(np.arange(half, dtype=np.float32) * np.float32(2.0 / HD)))
    freq = jnp.asarray(np.concatenate([freq, freq])[None, :], F32)
    operands = [queries, layer_input, w_key, w_value, grad_out, freq]
    if not exchange:
        operands.append(
            lax.all_to_all(layer_input, "seq", split_axis=1, concat_axis=0, tiled=True))
    width = depth // nf
    total = n * tok
    span = math.gcd(total, 1024)
    pieces = len(chunks_of(rows, 2 if n % 2 == 0 else 1))
    vmem = pltpu.VMEM
    dma = pltpu.SemaphoreType.DMA
    scratch = [vmem((depth, cols), BF16)] * 2
    scratch += [vmem((total, cols), BF16)] * 4
    scratch += [
        vmem((total, rows) if exchange else (16, 128), BF16),
        vmem((m_cols, HD), BF16), vmem((m_cols, HD), BF16), vmem((HD, m_cols), F32),
        vmem((total, m_cols), F32), vmem((total, m_cols), BF16), vmem((span, m_cols), BF16),
        vmem((8, m_cols), F32), vmem((8, m_cols), F32),
        vmem((HD, m_cols), F32), vmem((HD, m_cols), F32),
        vmem((span, cols), F32), vmem((span, cols), F32),
    ]
    scratch += [vmem((n, tok, cols), BF16)] * 4
    scratch += [vmem((tok, cols), F32)] * 4
    scratch += [
        vmem((2 * nf, tok, width), BF16), vmem((2 * nf, tok, width), BF16),
        vmem((nf, tok, width), F32),
    ]
    scratch += [dma((pieces, 3 * n)), dma((pieces, n))] * 2
    scratch += [dma((n,)), dma((n,))] * 4
    scratch += [dma((n,)), dma((n,)), dma((nf,)), dma((nf,))]
    scratch += [dma((n,)), dma((n,))] * 2
    scratch += [dma((2 * nf,)), dma((2 * nf,))]
    scratch += [vmem(queries.shape, BF16), vmem((tok, depth), BF16), vmem(queries.shape, BF16),
                dma((5,))]
    out_shape = [
        jax.ShapeDtypeStruct(queries.shape, BF16),
        jax.ShapeDtypeStruct(queries.shape, BF16),
        jax.ShapeDtypeStruct((tok, width), BF16),
        jax.ShapeDtypeStruct((rows, cols), F32),
        jax.ShapeDtypeStruct((rows, cols), F32),
    ]
    spec = pl.BlockSpec(memory_space=pltpu.VMEM)
    whole = pl.BlockSpec(memory_space=pl.ANY)
    results = pl.pallas_call(
        functools.partial(kernel, (n, nf, exchange)),
        out_shape=[pltpu.VMEM(o.shape, o.dtype) for o in out_shape],
        in_specs=[whole] * 5 + [spec] * (len(operands) - 5),
        out_specs=[spec] * len(out_shape),
        scratch_shapes=scratch,
        compiler_params=pltpu.CompilerParams(
            collective_id=0, has_side_effects=True, vmem_limit_bytes=60 * 1024 * 1024),
    )(*operands)
    return tuple(pl.pallas_call(
        publish,
        out_shape=out_shape,
        in_specs=[spec] * len(out_shape),
        out_specs=[whole] * len(out_shape),
        scratch_shapes=[dma((len(out_shape),))],
        compiler_params=pltpu.CompilerParams(vmem_limit_bytes=8 * 1024 * 1024),
    )(*results))


def solution(mesh):
    placed = (
        P("seq", "fsdp"),
        P("seq", None),
        P("seq", "fsdp"),
        P("seq", "fsdp"),
        P("seq", "fsdp"),
    )
    return jax.shard_map(
        functools.partial(body, mesh.shape["seq"], mesh.shape["fsdp"]),
        mesh=mesh,
        in_specs=placed,
        out_specs=(P("seq", "fsdp"),) * 5,
        check_vma=False,
    )
```

time: 68.7 us -> 73.9 us (1.076)
  Pallas kernels: 67.9 us -> 73.1 us
    pallas_call x1, Pallas kernels: 66.9 us -> 72.1 us  [body(): pl.pallas_call(functools.partial(kernel, (n, nf, exchange)), out_shape=[p...]
where the time goes in v1:
time: 73.9 us; the launch traced here: 73.7 us
  Pallas kernels  73.1 us (99%)
    pallas_call x1, Pallas kernels, body(): pl.pallas_call(functools.partial(kernel, (n, nf, exchange)), out_shape=[p...  72.1 us

profile of v1, /device:TPU:0, one launch (start us, length us, event | category | flops | bytes accessed | tf_op | source)
XLA Modules:
  0.0 73.7 jit_solution(2366970240092693895)
XLA Ops:
  0.6 72.1 %shard_map.101 = (bf16[128,512]{1,0:T(8,128)(2,1)S(1)}, bf16[128,512]{1,0:T(8,128)(2,1)S(1)}, bf16[128,1024]{1,0:T(8,128)(2,1)S(1)}, f32[512,128]{1,0:T(8,128)S(1)}, f32[512,128]{1,0:T(8,128)S(1)}) custom-call(bf16[128,512]{1,0:T(8,128)(2,1)} %refs_0_.1, bf16[128,4096]{1,0:T(8,128)(2,1)} %refs_1_.1, bf16[512,128]{1,0:T(8,128)(2,1)} %refs_2_.1, ...), custom_call_target="tpu_custom_call" | custom-call | tf_op jit(solution)/shard_map/pallas_call | solution.py:617
  72.7 1.0 %shard_map.102 = (bf16[128,512]{1,0:T(8,128)(2,1)}, bf16[128,512]{1,0:T(8,128)(2,1)}, bf16[128,1024]{1,0:T(8,128)(2,1)}, f32[512,128]{1,0:T(8,128)}, f32[512,128]{1,0:T(8,128)}) custom-call(bf16[128,512]{1,0:T(8,128)(2,1)S(1)} %get-tuple-element.10.refs_0_, bf16[128,512]{1,0:T(8,128)(2,1)S(1)} %get-tuple-element.11.refs_1_, ...), custom_call_target="tpu_custom_call" | custom-call | tf_op jit(solution)/shard_map/pallas_call | solution.py:626

commit v2 on v1

--- a/solution.py
+++ b/solution.py
@@ -41,19 +41,9 @@
     return ref.at[pl.ds(pl.multiple_of(b * size, size), size)]
 
 
-def chunks_of(rows, inner):
-    late = rows * 3 // 16 // 16 * 16 if inner == 2 else 0
-    rest = rows - late
-    pieces = 2 if rest >= 256 else 1
-    size = rest // pieces // 16 * 16
-    out, at = [], 0
-    for i in range(pieces):
-        count = size if i < pieces - 1 else rest - at
-        out.append((at, count, False))
-        at += count
-    if late:
-        out.append((at, late, True))
-    return out
+def pieces_of(rows, inner):
+    late = rows * 2 // 3 // 16 * 16 if inner == 2 else 0
+    return [(0, rows - late, False)] + ([(rows - late, late, True)] if late else [])
 
 
 def kernel(cfg, *refs):
@@ -66,7 +56,7 @@
     ao_ref, gq_ref, gi_ref, gwk_ref, gwv_ref = refs[:5]
     (wk_all, wv_all, k_all, v_all, dk_all, dv_all, x_all, q_st, g_st, g_tr,
      s_scr, p_scr, ds_scr, m_scr, l_scr, o_acc, dq_acc, dkp, dvp,
-     rk_send, rk_recv, rv_send, rv_recv, own_dk, own_dv, cos_scr, sin_scr,
+     rk_send, rk_recv, rv_send, rv_recv, own_dk, own_dv, sent_dk, sent_dv, cos_scr, sin_scr,
      gi_send, gi_recv, gi_own,
      wk_s, wk_r, wv_s, wv_r, k_s, k_r, v_s, v_r, dk_s, dk_r, dv_s, dv_r,
      x_s, x_r, xf_s, xf_r, rk_s, rk_r, rv_s, rv_r, gi_s, gi_r,
@@ -99,15 +89,17 @@
 
     barrier = pltpu.get_barrier_semaphore()
 
-    def greet_seq(d):
-        pl.semaphore_signal(
-            barrier, inc=1, device_id=((s + d) % n, f), device_id_type=MESH)
+    def greet(b):
+        pl.semaphore_signal(barrier, inc=1, device_id=(b, f), device_id_type=MESH)
 
     def greet_fsdp(d):
         pl.semaphore_signal(
             barrier, inc=1, device_id=(s, (f + d) % nf), device_id_type=MESH)
 
-    loop(1, n, greet_seq)
+    pl.when(z < outer - 1)(lambda: greet(s + inner))
+    pl.when(z > 0)(lambda: greet(s - inner))
+    if inner == 2:
+        greet(mate)
     loop(1, nf, greet_fsdp)
     loads = [
         pltpu.make_async_copy(src, dst, in_s.at[i])
@@ -124,79 +116,101 @@
         v_all[at, :] = jnp.zeros((tok, cols), BF16)
 
     loop(inner * (z + 1), n, clear)
-    pl.semaphore_wait(barrier, n + nf - 2)
+    pl.semaphore_wait(
+        barrier, jnp.minimum(z, 1) + jnp.minimum(outer - 1 - z, 1) + nf + inner - 2)
 
     class Gather:
         def __init__(self, ref, send, recv, causal=False):
             self.slot = lambda b: block_of(ref, b, tok)
-            self.send, self.recv = send, recv
-            self.give_to = outer - z if causal else outer
-            self.take_from = z + 1 if causal else outer
-
-        def outgoing(self, d):
-            return copy(self.slot(s), self.slot(s), self.send.at[d], self.recv.at[s],
-                        ((z + d) % outer * inner + y, f))
-
-        def to_mate(self):
-            return copy(self.slot(s), self.slot(s), self.send.at[0], self.recv.at[s], (mate, f))
+            self.send, self.recv, self.causal = send, recv, causal
+
+        def move(self, b, sem, level, row):
+            ref = self.slot(b)
+            return copy(ref, ref, self.send.at[sem], self.recv.at[b], (level * inner + row, f))
 
         def arrived(self, b):
-            copy(self.slot(b), self.slot(b), self.send.at[0], self.recv.at[b],
-                 (mate, f)).wait_recv()
-
-        def pass_on(self, d):
-            b = (z - d + outer) % outer * inner + y
-            return copy(self.slot(b), self.slot(b), self.send.at[outer + d], self.recv.at[b],
-                        (mate, f))
+            self.move(b, 0, z, y).wait_recv()
+
+        def ends(self):
+            return z == 0 if self.causal else jnp.logical_or(z == 0, z == outer - 1)
+
+        def sends(self, act):
+            if inner == 2:
+                getattr(self.move(s, outer, z, 1 - y), act)()
+
+            def near(d):
+                def up():
+                    getattr(self.move(s, z + d, z + d, y), act)()
+
+                def down():
+                    getattr(self.move(s, z - d, z - d, y), act)()
+
+                pl.when(z + d < outer)(up)
+                if not self.causal:
+                    pl.when(z >= d)(down)
+
+            loop(1, outer, near)
+            if inner == 2 and outer > 1:
+                pl.when(self.ends())(lambda: getattr(
+                    self.move(s, z, outer - 1 - z, 1 - y), act)())
 
         def start(self):
-            if inner == 2:
-                self.to_mate().start()
-            loop(1, self.give_to, lambda d: self.outgoing(d).start())
+            self.sends("start")
+
+        def relay(self, act):
+            def step(d):
+                def pass_on(level):
+                    b = level * inner + y
+                    if act == "start":
+                        self.arrived(b)
+                    if inner == 2:
+                        far = jnp.logical_or(level - z == outer - 1, z - level == outer - 1)
+                        pl.when(jnp.logical_not(far))(lambda: getattr(
+                            self.move(b, outer + 1 + level, z, 1 - y), act)())
+
+                pl.when(z >= d)(lambda: pass_on(z - d))
+                if not self.causal:
+                    pl.when(z + d < outer)(lambda: pass_on(z + d))
+
+            loop(1, outer, step)
 
         def forward(self):
-            def step(d):
-                self.arrived((z - d + outer) % outer * inner + y)
-                if inner == 2:
-                    self.pass_on(d).start()
-
-            loop(1, self.take_from, step)
+            self.relay("start")
 
         def finish(self):
             if inner == 2:
-                loop(0, self.take_from, lambda d: self.arrived(
-                    (z - d + outer) % outer * inner + (inner - 1 - y)))
+                loop(0, z + 1 if self.causal else outer,
+                     lambda level: self.arrived(level * inner + 1 - y))
 
         def drain(self):
-            if inner == 2:
-                self.to_mate().wait_send()
-            loop(1, self.give_to, lambda d: self.outgoing(d).wait_send())
-            if inner == 2:
-                loop(1, self.take_from, lambda d: self.pass_on(d).wait_send())
-
-    pieces = chunks_of(rows, inner)
+            self.sends("wait_send")
+            self.relay("wait_send")
+
+    pieces = pieces_of(rows, inner)
+
+    def is_end(level):
+        return jnp.logical_or(level == 0, level == outer - 1)
 
     class Weights:
         def __init__(self, ref, send, recv):
             self.ref, self.send, self.recv = ref, send, recv
 
         def hop(self, q, b, way):
-            at, count, _ = pieces[q]
+            at, count, late = pieces[q]
             ref = self.ref.at[pl.ds(pl.multiple_of(b * rows + at, 16), count)]
             dev = ((z + 1) * inner + y, (z - 1) * inner + y, mate)[way]
-            return copy(ref, ref, self.send.at[q, way * n + b], self.recv.at[q, b], (dev, f))
+            if late:
+                sem = 3 * outer + (2 * n + b // inner if way == 2 else way * n + b)
+            else:
+                sem = way * outer + b // inner
+            return copy(ref, ref, self.send.at[sem], self.recv.at[q * n + b], (dev, f))
 
         def arrived(self, q, b):
             self.hop(q, b, 2).wait_recv()
 
-        def order(self, way):
-            qs = list(range(len(pieces)))
-            return qs[::-1] if way == 2 else qs
-
-        def own(self, way, act):
+        def own(self, q, way, act):
             def go():
-                for q in self.order(way):
-                    getattr(self.hop(q, s, way), act)()
+                getattr(self.hop(q, s, way), act)()
 
             if way == 0:
                 pl.when(z < outer - 1)(go)
@@ -208,59 +222,76 @@
         def mates(self, act):
             for q, (_, _, late) in enumerate(pieces):
                 if late:
-                    if act == "start":
-                        self.arrived(q, mate)
-                    pl.when(z < outer - 1)(lambda q=q: getattr(self.hop(q, mate, 0), act)())
-                    pl.when(z > 0)(lambda q=q: getattr(self.hop(q, mate, 1), act)())
-
-        def relay(self, d, way, act):
-            level = z - d if way == 0 else z + d
-            more = z < outer - 1 if way == 0 else z > 0
-            for q, (_, _, late) in enumerate(pieces):
-                for line in range(inner) if late else (y,):
-                    b = level * inner + line
-                    if act == "start":
-                        self.arrived(q, b)
-                    pl.when(more)(lambda q=q, b=b: getattr(self.hop(q, b, way), act)())
-                    if inner == 2 and not late:
-                        getattr(self.hop(q, b, 2), act)()
-
-        def relays(self, act, after=None):
-            if after is not None:
-                pl.when(z == 0)(lambda: after(0))
-                pl.when(z == outer - 1)(lambda: after(1))
-            self.mates(act)
-
-            def step(d):
-                @pl.when(z >= d)
-                def _():
-                    self.relay(d, 0, act)
-                    if after is not None:
-                        pl.when(z == d)(lambda: after(0))
-
-                @pl.when(z + d < outer)
-                def _():
-                    self.relay(d, 1, act)
-                    if after is not None:
-                        pl.when(z + d == outer - 1)(lambda: after(1))
-
-            loop(1, outer, step)
-            if after is not None:
-                after(2)
+                    @pl.when(is_end(z))
+                    def _(q=q):
+                        if act == "start":
+                            self.arrived(q, mate)
+                        pl.when(z < outer - 1)(lambda: getattr(self.hop(q, mate, 0), act)())
+                        pl.when(z > 0)(lambda: getattr(self.hop(q, mate, 1), act)())
+
+        def relay(self, q, d, act):
+            late = pieces[q][2]
+
+            def one(b, way, to_mate):
+                more = z < outer - 1 if way == 0 else z > 0
+                if act == "start":
+                    self.arrived(q, b)
+                pl.when(more)(lambda: getattr(self.hop(q, b, way), act)())
+                if to_mate:
+                    getattr(self.hop(q, b, 2), act)()
+
+            def pass_on(level, way):
+                if late:
+                    end = is_end(level)
+
+                    @pl.when(end)
+                    def _():
+                        for line in range(inner):
+                            one(level * inner + line, way, False)
+
+                    pl.when(jnp.logical_not(end))(lambda: one(level * inner + y, way, True))
+                else:
+                    one(level * inner + y, way, inner == 2)
+
+            pl.when(z >= d)(lambda: pass_on(z - d, 0))
+            pl.when(z + d < outer)(lambda: pass_on(z + d, 1))
 
         def finish(self):
             if inner == 2:
                 def step(level):
                     for q, (_, _, late) in enumerate(pieces):
-                        if not late:
-                            self.arrived(q, level * inner + (inner - 1 - y))
+                        def go(q=q):
+                            self.arrived(q, level * inner + (1 - y))
+
+                        if late:
+                            pl.when(jnp.logical_not(is_end(level)))(go)
+                        else:
+                            go()
 
                 loop(0, outer, step)
 
-        def drain(self):
-            for way in range(3):
-                self.own(way, "wait_send")
-            self.relays("wait_send")
+    def move_weights(act):
+        gathers = (wk_gather, wv_gather)
+        last = len(pieces) - 1
+        for way in (0, 1):
+            for gather in gathers:
+                for q in range(len(pieces)):
+                    gather.own(q, way, act)
+        for q in range(last, -1, -1):
+            for gather in gathers:
+                gather.own(q, 2, act)
+
+    def relay_weights(act):
+        gathers = (wk_gather, wv_gather)
+        for gather in gathers:
+            gather.mates(act)
+
+        def step(d):
+            for q in range(len(pieces)):
+                for gather in gathers:
+                    gather.relay(q, d, act)
+
+        loop(1, outer, step)
 
     wk_gather = Weights(wk_all, wk_s, wk_r)
     wv_gather = Weights(wv_all, wv_s, wv_r)
@@ -270,9 +301,9 @@
     dv_gather = Gather(dv_all, dv_s, dv_r)
 
     loads[0].wait()
-    for way in (0, 1, 2):
-        wk_gather.own(way, "start")
-    for load in loads[1:]:
+    loads[1].wait()
+    move_weights("start")
+    for load in loads[2:]:
         load.wait()
 
     own_rows = pl.ds(pl.multiple_of(s * tok, tok), tok)
@@ -315,7 +346,7 @@
     cos_scr[...] = jnp.cos(angle)
     sin_scr[...] = jnp.where(lane < HD // 2, -jnp.sin(angle), jnp.sin(angle))
 
-    wk_gather.relays("start", lambda way: wv_gather.own(way, "start"))
+    relay_weights("start")
     wk_gather.finish()
 
     lin = dot_nn(x_ref[...], wk_all[...])
@@ -323,15 +354,14 @@
     k_all[own_rows, :] = turned.astype(BF16)
     k_gather.start()
 
-    wv_gather.relays("start")
-    k_gather.forward()
+    if exchange:
+        loop(0, s, lambda b: x_copy(b).start())
     wv_gather.finish()
     v_all[own_rows, :] = dot_nn(x_ref[...], wv_all[...]).astype(BF16)
     v_gather.start()
-    if exchange:
-        loop(0, s, lambda b: x_copy(b).start())
+    k_gather.forward()
+    v_gather.forward()
     k_gather.finish()
-
     def each_span(step):
         if spans == 1:
             step(0)
@@ -372,25 +402,83 @@
     each_span(weigh)
     inverse = 1.0 / jnp.sum(l_scr[...], axis=0, keepdims=True)
 
-    def rs_copy(send, recv, send_sem, recv_sem, j):
-        return copy(send.at[j], recv.at[s], send_sem.at[j], recv_sem.at[s], (j, f))
-
-    def rk_copy(j):
-        return rs_copy(rk_send, rk_recv, rk_s, rk_r, j)
-
-    def rv_copy(j):
-        return rs_copy(rv_send, rv_recv, rv_s, rv_r, j)
-
-    def hand_out(base, low, high, partial, own, start):
+    half = n // 2 if n % 2 == 0 else 0
+    low_end = s // half * half if half else 0
+
+    class Reduce:
+        def __init__(self, send, recv, send_sem, recv_sem, own, sent):
+            self.send, self.recv, self.send_sem, self.recv_sem = send, recv, send_sem, recv_sem
+            self.own, self.sent = own, sent
+
+        def direct(self, j):
+            return copy(self.send.at[j], self.recv.at[s], self.send_sem.at[j], self.recv_sem.at[s],
+                        (j, f))
+
+        def inward(self, j):
+            slot = n + s - half
+            return copy(self.send.at[j], self.recv.at[slot], self.send_sem.at[j],
+                        self.recv_sem.at[slot], (j + half, f))
+
+        def got(self, slot):
+            copy(self.send.at[0], self.recv.at[slot], self.send_sem.at[0], self.recv_sem.at[slot],
+                 (mate, f)).wait_recv()
+            return self.recv[slot].astype(F32)
+
+        def hand(self, low, high, act):
+            high = jnp.minimum(high, s)
+            loop(jnp.maximum(low, low_end), high, lambda j: getattr(self.direct(j), act)())
+            if half:
+                @pl.when(s >= half)
+                def _():
+                    loop(low, jnp.minimum(high, half), lambda j: pl.when(j + half != s)(
+                        lambda: getattr(self.inward(j), act)()))
+
+        def pass_on(self):
+            if half:
+                @pl.when(s >= half)
+                def _():
+                    def add(i):
+                        self.sent[...] += self.got(n + i - half)
+
+                    loop(half, s, add)
+                    loop(s + 1, n, add)
+                    self.send[s - half] = self.sent[...].astype(BF16)
+                    self.direct(s - half).start()
+
+        def take(self):
+            def add(j):
+                self.own[...] += self.got(j)
+
+            loop(s + 1, low_end + half if half else n, add)
+            if half:
+                pl.when(s < half)(lambda: add(s + half))
+
+        def drain(self):
+            self.hand(0, n, "wait_send")
+            if half:
+                pl.when(s >= half)(lambda: self.direct(s - half).wait_send())
+
+    rk = Reduce(rk_send, rk_recv, rk_s, rk_r, own_dk, sent_dk)
+    rv = Reduce(rv_send, rv_recv, rv_s, rv_r, own_dv, sent_dv)
+
+    def hand_out(base, low, high, partial, reduce):
         first = base // tok
-        loop(first + low, jnp.minimum(first + high, s), start)
+        reduce.hand(first + low, first + high, "start")
+
+        def keep(block, out):
+            at = pl.ds(pl.multiple_of((block - first) * tok, tok), tok)
+            out[...] = partial[at, :]
+
         if spans == 1:
             if high == per_span:
-                own[...] = partial[own_rows, :]
+                keep(s, reduce.own)
+                if half:
+                    pl.when(s >= half)(lambda: keep(s - half, reduce.sent))
         else:
-            @pl.when(jnp.logical_and(s >= first + low, s < first + high))
-            def _():
-                own[...] = partial[pl.ds(pl.multiple_of(s * tok - base, tok), tok), :]
+            for block, out in ((s, reduce.own), (s - half, reduce.sent)):
+                @pl.when(jnp.logical_and(block >= first + low, block < first + high))
+                def _(block=block, out=out):
+                    keep(block, out)
 
     def store_parts(base, c, value, partial, send):
         partial[c * chunk:(c + 1) * chunk, :] = value
@@ -404,12 +492,9 @@
             low = p.astype(BF16)
             p_scr[at_chunk(base, c), :] = low
             store_parts(base, c, dot_nn(low, g_st[...]), dvp, rv_send)
-        hand_out(base, 0, per_span, dvp, own_dv, lambda j: rv_copy(j).start())
+        hand_out(base, 0, per_span, dvp, rv)
 
     each_span(value_part)
-    v_gather.forward()
-    if exchange:
-        loop(s + 1, n, lambda b: x_copy(b).start())
     v_gather.finish()
 
     def weighted(base):
@@ -421,14 +506,13 @@
     def key_part(base):
         halves = 2 if (span // chunk) % 2 == 0 else 1
         count = span // chunk // halves
-        for half in range(halves):
-            for c in range(half * count, (half + 1) * count):
+        for part_of in range(halves):
+            for c in range(part_of * count, (part_of + 1) * count):
                 dp = dot_nt(v_all[at_chunk(base, c), :], g_st[...])
                 ds = (s_scr[at_chunk(base, c), :] * (dp - delta)).astype(BF16)
                 ds_scr[c * chunk:(c + 1) * chunk, :] = ds
                 store_parts(base, c, dot_nn(ds, q_st[...]), dkp, rk_send)
-            hand_out(base, half * per_span // halves, (half + 1) * per_span // halves, dkp, own_dk,
-                     lambda j: rk_copy(j).start())
+            hand_out(base, part_of * per_span // halves, (part_of + 1) * per_span // halves, dkp, rk)
         dq_acc[...] += dot_tn(k_all[pl.ds(base, span), :], ds_scr[...])
 
     each_span(key_part)
@@ -438,31 +522,23 @@
         gq_ref[:, g * HD:(g + 1) * HD] = (dq_acc[:, at] * scale).T.astype(BF16)
 
     if exchange:
+        loop(s + 1, n, lambda b: x_copy(b).start())
+
+    rv.pass_on()
+    rv.take()
+    dv_all[own_rows, :] = own_dv[...].astype(BF16)
+    dv_gather.start()
+    rk.pass_on()
+    if exchange:
         loop(0, s, x_arrived)
         loop(s + 1, n, x_arrived)
         loop(1, nf, lambda d: xf_copy(d).start())
-
-    def take(recv, make, own):
-        def step(j):
-            make(j).wait_recv()
-            own[...] += recv[j].astype(F32)
-
-        loop(s + 1, n, step)
-
-    def rv_from(j):
-        return copy(rv_send.at[0], rv_recv.at[j], rv_s.at[0], rv_r.at[j], (mate, f))
-
-    def rk_from(j):
-        return copy(rk_send.at[0], rk_recv.at[j], rk_s.at[0], rk_r.at[j], (mate, f))
-
-    take(rv_recv, rv_from, own_dv)
-    dv_all[own_rows, :] = own_dv[...].astype(BF16)
-    dv_gather.start()
-    take(rk_recv, rk_from, own_dk)
+    rk.take()
     lin = own_dk[...] * scale
     turned = lin * cos_scr[...] - pltpu.roll(lin, HD // 2, 1) * sin_scr[...]
     dk_all[own_rows, :] = turned.astype(BF16)
     dk_gather.start()
+    dv_gather.forward()
 
     def input_term(b):
         at = pl.ds(pl.multiple_of(b * width, width), width)
@@ -502,12 +578,16 @@
         gi_send[chips + d] = gi_own[(chip + d) % chips].astype(BF16)
         gi_far(d).start()
 
+    def far_terms(d):
+        if cores == 2:
+            twin_term(d)
+        own_term(d)
+        far_term(d)
+
+    loop(1, chips, far_terms)
     if cores == 2:
-        loop(1, chips + 1, twin_term)
-    loop(1, chips + 1, own_term)
-    loop(1, chips, far_term)
-    if cores == 2:
-        join(0)
+        twin_term(0)
+    own_term(0)
 
     def weight_grad(grads, out):
         if exchange:
@@ -520,7 +600,6 @@
                 grad = term if grad is None else grad + term
             out[...] = grad
 
-    dv_gather.forward()
     dk_gather.forward()
     dv_gather.finish()
     if exchange:
@@ -535,17 +614,21 @@
              gi_r.at[chips + b], (s, b * cores + core)).wait_recv()
         gi_own[chip] += gi_recv[chips + b].astype(F32)
 
+    if cores == 2:
+        join(0)
     loop(1, chips, gi_take)
     gi_ref[...] = gi_own[chip].astype(BF16)
 
-    for gather in (wk_gather, wv_gather, k_gather, v_gather, dk_gather, dv_gather):
+    move_weights("wait_send")
+    relay_weights("wait_send")
+    for gather in (k_gather, v_gather, dk_gather, dv_gather):
         gather.drain()
     if exchange:
         loop(0, s, lambda b: x_copy(b).wait_send())
         loop(s + 1, n, lambda b: x_copy(b).wait_send())
         loop(1, nf, lambda d: xf_copy(d).wait_send())
-    loop(0, s, lambda j: rv_copy(j).wait_send())
-    loop(0, s, lambda j: rk_copy(j).wait_send())
+    rv.drain()
+    rk.drain()
     if cores == 2:
         loop(0, chips, lambda o: gi_twin(o).wait_send())
     loop(1, chips, lambda d: gi_far(d).wait_send())
@@ -579,7 +662,10 @@
     width = depth // nf
     total = n * tok
     span = math.gcd(total, 1024)
-    pieces = len(chunks_of(rows, 2 if n % 2 == 0 else 1))
+    inner = 2 if n % 2 == 0 else 1
+    outer = n // inner
+    pieces = len(pieces_of(rows, inner))
+    hops = 3 * outer + (2 * n + outer if pieces > 1 else 0)
     vmem = pltpu.VMEM
     dma = pltpu.SemaphoreType.DMA
     scratch = [vmem((depth, cols), BF16)] * 2
@@ -592,16 +678,17 @@
         vmem((HD, m_cols), F32), vmem((HD, m_cols), F32),
         vmem((span, cols), F32), vmem((span, cols), F32),
     ]
-    scratch += [vmem((n, tok, cols), BF16)] * 4
-    scratch += [vmem((tok, cols), F32)] * 4
+    slots = n + n // 2
+    scratch += [vmem((n, tok, cols), BF16), vmem((slots, tok, cols), BF16)] * 2
+    scratch += [vmem((tok, cols), F32)] * 6
     scratch += [
         vmem((2 * nf, tok, width), BF16), vmem((2 * nf, tok, width), BF16),
         vmem((nf, tok, width), F32),
     ]
-    scratch += [dma((pieces, 3 * n)), dma((pieces, n))] * 2
-    scratch += [dma((n,)), dma((n,))] * 4
+    scratch += [dma((hops,)), dma((pieces * n,))] * 2
+    scratch += [dma((2 * outer + 1,)), dma((n,))] * 4
     scratch += [dma((n,)), dma((n,)), dma((nf,)), dma((nf,))]
-    scratch += [dma((n,)), dma((n,))] * 2
+    scratch += [dma((n,)), dma((slots,))] * 2
     scratch += [dma((2 * nf,)), dma((2 * nf,))]
     scratch += [vmem(queries.shape, BF16), vmem((tok, depth), BF16), vmem(queries.shape, BF16),
                 dma((5,))]

time: 73.9 us -> 66 us (0.89)
  Pallas kernels: 73.1 us -> 65.2 us
    pallas_call x1, Pallas kernels: 72.1 us -> 64.2 us  [body(): pl.pallas_call(functools.partial(kernel, (n, nf, exchange)), out_shape=[p...]
where the time goes in v2:
time: 66 us; the launch traced here: 65.8 us
  Pallas kernels  65.2 us (99%)
    pallas_call x1, Pallas kernels, body(): pl.pallas_call(functools.partial(kernel, (n, nf, exchange)), out_shape=[p...  64.2 us

profile of v2, /device:TPU:0, one launch (start us, length us, event | category | flops | bytes accessed | tf_op | source)
XLA Modules:
  0.0 65.8 jit_solution(17817644388346881047)
XLA Ops:
  0.6 64.2 %shard_map.101 = (bf16[128,512]{1,0:T(8,128)(2,1)S(1)}, bf16[128,512]{1,0:T(8,128)(2,1)S(1)}, bf16[128,1024]{1,0:T(8,128)(2,1)S(1)}, f32[512,128]{1,0:T(8,128)S(1)}, f32[512,128]{1,0:T(8,128)S(1)}) custom-call(bf16[128,512]{1,0:T(8,128)(2,1)} %refs_0_.1, bf16[128,4096]{1,0:T(8,128)(2,1)} %refs_1_.1, bf16[512,128]{1,0:T(8,128)(2,1)} %refs_2_.1, ...), custom_call_target="tpu_custom_call" | custom-call | tf_op jit(solution)/shard_map/pallas_call | solution.py:704
  64.8 1.0 %shard_map.102 = (bf16[128,512]{1,0:T(8,128)(2,1)}, bf16[128,512]{1,0:T(8,128)(2,1)}, bf16[128,1024]{1,0:T(8,128)(2,1)}, f32[512,128]{1,0:T(8,128)}, f32[512,128]{1,0:T(8,128)}) custom-call(bf16[128,512]{1,0:T(8,128)(2,1)S(1)} %get-tuple-element.10.refs_0_, bf16[128,512]{1,0:T(8,128)(2,1)S(1)} %get-tuple-element.11.refs_1_, ...), custom_call_target="tpu_custom_call" | custom-call | tf_op jit(solution)/shard_map/pallas_call | solution.py:713

commit v3 on v2

--- a/solution.py
+++ b/solution.py
@@ -42,7 +42,7 @@
 
 
 def pieces_of(rows, inner):
-    late = rows * 2 // 3 // 16 * 16 if inner == 2 else 0
+    late = rows * 5 // 8 // 16 * 16 if inner == 2 else 0
     return [(0, rows - late, False)] + ([(rows - late, late, True)] if late else [])
 
 
@@ -57,8 +57,8 @@
     (wk_all, wv_all, k_all, v_all, dk_all, dv_all, x_all, q_st, g_st, g_tr,
      s_scr, p_scr, ds_scr, m_scr, l_scr, o_acc, dq_acc, dkp, dvp,
      rk_send, rk_recv, rv_send, rv_recv, own_dk, own_dv, sent_dk, sent_dv, cos_scr, sin_scr,
-     gi_send, gi_recv, gi_own,
-     wk_s, wk_r, wv_s, wv_r, k_s, k_r, v_s, v_r, dk_s, dk_r, dv_s, dv_r,
+     gi_send, gi_recv, gi_own, xg, pe_send, pe_recv,
+     told, xe_s, xe_r, pe_s, pe_r, wk_s, wk_r, wv_s, wv_r, k_s, k_r, v_s, v_r, dk_s, dk_r, dv_s, dv_r,
      x_s, x_r, xf_s, xf_r, rk_s, rk_r, rv_s, rv_r, gi_s, gi_r,
      q_ref, x_ref, g_ref, in_s) = refs[5:]
     tok = x_ref.shape[0]
@@ -80,6 +80,13 @@
     z = s // inner
     y = s % inner
     mate = z * inner + (inner - 1 - y)
+    last = outer - 1
+    hosted = exchange and inner == 2 and outer >= 4
+    cores = 2 if nf % 2 == 0 else 1
+    chips = nf // cores
+    chip = f // cores
+    core = f % cores
+    twin = chip * cores + (cores - 1 - core)
 
     def copy(src, dst, send, recv, dev):
         return pltpu.make_async_remote_copy(
@@ -135,29 +142,35 @@
             return z == 0 if self.causal else jnp.logical_or(z == 0, z == outer - 1)
 
         def sends(self, act):
-            if inner == 2:
-                getattr(self.move(s, outer, z, 1 - y), act)()
+            def run(sem, level, row):
+                getattr(self.move(s, sem, level, row), act)()
 
             def near(d):
-                def up():
-                    getattr(self.move(s, z + d, z + d, y), act)()
-
-                def down():
-                    getattr(self.move(s, z - d, z - d, y), act)()
-
-                pl.when(z + d < outer)(up)
+                pl.when(z + d < outer)(lambda: run(z + d, z + d, y))
                 if not self.causal:
-                    pl.when(z >= d)(down)
-
-            loop(1, outer, near)
-            if inner == 2 and outer > 1:
-                pl.when(self.ends())(lambda: getattr(
-                    self.move(s, z, outer - 1 - z, 1 - y), act)())
+                    pl.when(z >= d)(lambda: run(z - d, z - d, y))
+
+            def far():
+                if inner == 2 and outer > 1:
+                    pl.when(self.ends())(lambda: run(z, outer - 1 - z, 1 - y))
+
+            def to_mate():
+                if inner == 2:
+                    run(outer, z, 1 - y)
+
+            if self.causal:
+                far()
+                loop(0, outer - 1, lambda i: near(outer - 1 - i))
+                to_mate()
+            else:
+                to_mate()
+                loop(1, outer, near)
+                far()
 
         def start(self):
             self.sends("start")
 
-        def relay(self, act):
+        def relay(self, act, low=1, high=outer):
             def step(d):
                 def pass_on(level):
                     b = level * inner + y
@@ -172,10 +185,10 @@
                 if not self.causal:
                     pl.when(z + d < outer)(lambda: pass_on(z + d))
 
-            loop(1, outer, step)
-
-        def forward(self):
-            self.relay("start")
+            loop(low, high, step)
+
+        def forward(self, low=1, high=outer):
+            self.relay("start", low, high)
 
         def finish(self):
             if inner == 2:
@@ -192,8 +205,8 @@
         return jnp.logical_or(level == 0, level == outer - 1)
 
     class Weights:
-        def __init__(self, ref, send, recv):
-            self.ref, self.send, self.recv = ref, send, recv
+        def __init__(self, ref, send, recv, deferred=False):
+            self.ref, self.send, self.recv, self.deferred = ref, send, recv, deferred
 
         def hop(self, q, b, way):
             at, count, late = pieces[q]
@@ -233,7 +246,11 @@
             late = pieces[q][2]
 
             def one(b, way, to_mate):
-                more = z < outer - 1 if way == 0 else z > 0
+                more = z < last if way == 0 else z > 0
+                if self.deferred:
+                    more = jnp.logical_and(more, jnp.logical_not(
+                        jnp.logical_and(z == last - 1, b // inner == 0) if way == 0
+                        else jnp.logical_and(z == 1, b // inner == last)))
                 if act == "start":
                     self.arrived(q, b)
                 pl.when(more)(lambda: getattr(self.hop(q, b, way), act)())
@@ -256,7 +273,16 @@
             pl.when(z >= d)(lambda: pass_on(z - d, 0))
             pl.when(z + d < outer)(lambda: pass_on(z + d, 1))
 
-        def finish(self):
+        def held(self, way, act):
+            def run():
+                for q, (_, _, late) in enumerate(pieces):
+                    for line in range(inner) if late else (y,):
+                        level = last if way == 1 else 0
+                        getattr(self.hop(q, level * inner + line, way), act)()
+
+            pl.when(z == (1 if way == 1 else last - 1))(run)
+
+        def finish(self, low=0, high=outer):
             if inner == 2:
                 def step(level):
                     for q, (_, _, late) in enumerate(pieces):
@@ -268,42 +294,117 @@
                         else:
                             go()
 
-                loop(0, outer, step)
+                loop(low, high, step)
 
     def move_weights(act):
-        gathers = (wk_gather, wv_gather)
-        last = len(pieces) - 1
-        for way in (0, 1):
-            for gather in gathers:
+        for gather in (wk_gather, wv_gather):
+            for q in range(len(pieces)):
+                gather.own(q, 0, act)
+                gather.own(q, 1, act)
+            for q in range(len(pieces) - 1, -1, -1):
+                gather.own(q, 2, act)
+            gather.mates(act)
+
+    def relay_weights(act, low, high):
+        def step(d):
+            for gather in (wk_gather, wv_gather):
                 for q in range(len(pieces)):
-                    gather.own(q, way, act)
-        for q in range(last, -1, -1):
-            for gather in gathers:
-                gather.own(q, 2, act)
-
-    def relay_weights(act):
-        gathers = (wk_gather, wv_gather)
-        for gather in gathers:
-            gather.mates(act)
-
-        def step(d):
-            for q in range(len(pieces)):
-                for gather in gathers:
                     gather.relay(q, d, act)
 
-        loop(1, outer, step)
+        loop(low, high, step)
+
+    def when_host(act):
+        pl.when(jnp.logical_or(z == 1, z == last - 1))(act)
+
+    class Guest:
+        def __init__(self):
+            self.span = inner * rows
+            self.part = self.span // nf
+
+        def place(self, p):
+            return xg.at[:, pl.ds(pl.multiple_of(p * self.part, 128), self.part)]
+
+        def move(self, p, sem, dev):
+            return copy(self.place(p), self.place(p), xe_s.at[sem], xe_r.at[p], dev)
+
+        def arrived(self, p):
+            self.move(p, 0, (s, f)).wait_recv()
+
+        def leave(self, act):
+            @pl.when(is_end(z))
+            def _():
+                host = jnp.minimum(jnp.maximum(z, 1), last - 1) * inner + y
+                at = pl.multiple_of((last - z) * self.span + f * self.part, 128)
+                getattr(copy(x_ref.at[:, pl.ds(at, self.part)], self.place(f), xe_s.at[0],
+                             xe_r.at[f], (host, f)), act)()
+
+        def spread(self, act):
+            def run():
+                if act == "start":
+                    self.arrived(f)
+                loop(1, chips, lambda d: getattr(self.move(
+                    f, d, (s, (chip + d) % chips * cores + core)), act)())
+                if cores == 2:
+                    getattr(self.move(f, chips + chip, (s, twin)), act)()
+
+            when_host(run)
+
+        def share(self, act):
+            def step(d):
+                o = (chip + d) % chips
+                if act == "start":
+                    self.arrived(o * cores + core)
+                if cores == 2:
+                    getattr(self.move(o * cores + core, chips + o, (s, twin)), act)()
+
+            when_host(lambda: loop(1, chips, step))
+
+        def finish(self):
+            if cores == 2:
+                loop(0, chips, lambda o: self.arrived(o * cores + 1 - core))
+
+        def reply(self, i):
+            end = jnp.minimum(z - 1, 1) * last
+            return copy(pe_send.at[i], pe_recv.at[i], pe_s.at[i], pe_r.at[i], (end * inner + y, f))
+
+        def partial(self, i, weights):
+            def run():
+                at = (last - jnp.minimum(z - 1, 1) * last) * self.span
+                w = weights[pl.ds(pl.multiple_of(at, 16), self.span), :]
+                pe_send[i] = dot_nn(xg[...], w).astype(BF16)
+                self.reply(i).start()
+
+            when_host(run)
+
+        def rest(self, weights):
+            at = pl.multiple_of(z // last * self.span, 128)
+            here = pl.ds(at, (outer - 1) * self.span)
+            return dot_nn(x_ref[:, here], weights[here, :])
+
+        def returned(self, i):
+            copy(pe_send.at[i], pe_recv.at[i], pe_s.at[i], pe_r.at[i], (mate, f)).wait_recv()
+            return pe_recv[i].astype(F32)
+
+        def drain(self):
+            self.leave("wait_send")
+            self.spread("wait_send")
+            self.share("wait_send")
+            when_host(lambda: loop(0, 2, lambda i: self.reply(i).wait_send()))
 
     wk_gather = Weights(wk_all, wk_s, wk_r)
-    wv_gather = Weights(wv_all, wv_s, wv_r)
+    wv_gather = Weights(wv_all, wv_s, wv_r, deferred=hosted)
+    guests = Guest() if hosted else None
     k_gather = Gather(k_all, k_s, k_r, causal=True)
     v_gather = Gather(v_all, v_s, v_r, causal=True)
-    dk_gather = Gather(dk_all, dk_s, dk_r)
-    dv_gather = Gather(dv_all, dv_s, dv_r)
-
-    loads[0].wait()
-    loads[1].wait()
+    dk_gather = Gather(dk_all, *((v_s, v_r) if exchange else (dk_s, dk_r)))
+    dv_gather = Gather(dv_all, *((k_s, k_r) if exchange else (dv_s, dv_r)))
+
+    for load in loads[:3]:
+        load.wait()
+    if hosted:
+        guests.leave("start")
     move_weights("start")
-    for load in loads[2:]:
+    for load in loads[3:]:
         load.wait()
 
     own_rows = pl.ds(pl.multiple_of(s * tok, tok), tok)
@@ -346,21 +447,95 @@
     cos_scr[...] = jnp.cos(angle)
     sin_scr[...] = jnp.where(lane < HD // 2, -jnp.sin(angle), jnp.sin(angle))
 
-    relay_weights("start")
-    wk_gather.finish()
-
-    lin = dot_nn(x_ref[...], wk_all[...])
-    turned = lin * cos_scr[...] + pltpu.roll(lin, HD // 2, 1) * sin_scr[...]
-    k_all[own_rows, :] = turned.astype(BF16)
-    k_gather.start()
-
+    def tell(which, device):
+        pl.semaphore_signal(
+            told.at[which], inc=1, device_id=(device, f), device_id_type=MESH)
+
+    if hosted:
+        pl.when(z < last - 1)(lambda: pl.semaphore_wait(told.at[0], 1))
+        pl.when(jnp.logical_and(z > 0, z < last))(lambda: tell(0, s - inner))
+
+        @pl.when(z == 0)
+        def _():
+            tell(1, mate)
+            pl.semaphore_wait(told.at[1], 1)
+
+    relay_weights("start", 1, 2)
+    if hosted:
+        guests.spread("start")
+    relay_weights("start", 2, outer - 1)
+    if hosted:
+        guests.share("start")
+    def x_ahead():
+        loop(inner * (z + 1), n, lambda b: x_copy(b).start())
+
+    if hosted:
+        pl.when(z == 0)(x_ahead)
+
+    def last_relays(act, gathers):
+        for gather in gathers:
+            for q in range(len(pieces)):
+                gather.relay(q, outer - 1, act)
+
+    def rotated(lin):
+        return lin * cos_scr[...] + pltpu.roll(lin, HD // 2, 1) * sin_scr[...]
+
+    def finish_levels(low, high):
+        wk_gather.finish(low, high)
+        wv_gather.finish(low, high)
+
+    def keep_keys(lin):
+        k_all[own_rows, :] = rotated(lin).astype(BF16)
+        k_gather.start()
+
+    def keep_values(value):
+        v_all[own_rows, :] = value.astype(BF16)
+        v_gather.start()
+
+    def project():
+        keep_keys(dot_nn(x_ref[...], wk_all[...]))
+        keep_values(dot_nn(x_ref[...], wv_all[...]))
+
+    def project_end():
+        first = jnp.minimum(z, 1)
+        with jax.named_scope("wkfin"):
+            finish_levels(first, first + outer - 1)
+        with jax.named_scope("kproj"):
+            keys, values = guests.rest(wk_all), guests.rest(wv_all)
+        with jax.named_scope("xfin"):
+            keep_keys(keys + guests.returned(0))
+        with jax.named_scope("vproj"):
+            keep_values(values + guests.returned(1))
+
+    def project_inner():
+        with jax.named_scope("wkfin"):
+            finish_levels(0, outer)
+        with jax.named_scope("xfin"):
+            pl.when(z < last - 1)(x_ahead)
+            when_host(guests.finish)
+        with jax.named_scope("kproj"):
+            guests.partial(0, wk_all)
+            guests.partial(1, wv_all)
+        with jax.named_scope("vproj"):
+            project()
+
+    if hosted:
+        pl.when(is_end(z))(project_end)
+        pl.when(jnp.logical_not(is_end(z)))(project_inner)
+    else:
+        if outer > 1:
+            last_relays("start", (wk_gather, wv_gather))
+        finish_levels(0, outer)
+        project()
+    if hosted:
+        wv_gather.held(1, "start")
     if exchange:
+        pl.when(z == last - 1)(x_ahead) if hosted else x_ahead()
         loop(0, s, lambda b: x_copy(b).start())
-    wv_gather.finish()
-    v_all[own_rows, :] = dot_nn(x_ref[...], wv_all[...]).astype(BF16)
-    v_gather.start()
     k_gather.forward()
     v_gather.forward()
+    if hosted:
+        last_relays("start", (wk_gather,))
     k_gather.finish()
     def each_span(step):
         if spans == 1:
@@ -496,6 +671,8 @@
 
     each_span(value_part)
     v_gather.finish()
+    if exchange:
+        loop(s + 1, inner * (z + 1), lambda b: x_copy(b).start())
 
     def weighted(base):
         o_acc[...] += dot_tn(v_all[pl.ds(base, span), :], p_scr[pl.ds(base, span), :])
@@ -516,40 +693,55 @@
         dq_acc[...] += dot_tn(k_all[pl.ds(base, span), :], ds_scr[...])
 
     each_span(key_part)
+    if hosted:
+        wv_gather.held(0, "start")
     for g in range(group):
         at = slice(g * tok, (g + 1) * tok)
         ao_ref[:, g * HD:(g + 1) * HD] = o_acc[:, at].T.astype(BF16)
         gq_ref[:, g * HD:(g + 1) * HD] = (dq_acc[:, at] * scale).T.astype(BF16)
 
-    if exchange:
-        loop(s + 1, n, lambda b: x_copy(b).start())
-
-    rv.pass_on()
-    rv.take()
-    dv_all[own_rows, :] = own_dv[...].astype(BF16)
-    dv_gather.start()
-    rk.pass_on()
+
     if exchange:
         loop(0, s, x_arrived)
         loop(s + 1, n, x_arrived)
         loop(1, nf, lambda d: xf_copy(d).start())
+    def drain_early():
+        move_weights("wait_send")
+        relay_weights("wait_send", 1, outer)
+        if hosted:
+            for way in (0, 1):
+                wv_gather.held(way, "wait_send")
+            guests.drain()
+        if exchange:
+            loop(0, s, lambda b: x_copy(b).wait_send())
+            loop(s + 1, n, lambda b: x_copy(b).wait_send())
+
+    for gather in (k_gather, v_gather):
+        gather.drain()
+    rv.pass_on()
+    rk.pass_on()
+    @pl.when(z < outer // 2)
+    def _():
+        if hosted:
+            pl.when(z == 0)(lambda: last_relays("start", (wv_gather,)))
+        drain_early()
+
+    if hosted:
+        pl.when(z > outer // 2)(lambda: pl.semaphore_wait(told.at[0], 1))
+        pl.when(jnp.logical_and(z >= outer // 2, z < last))(lambda: tell(0, s + inner))
+    rv.take()
+    dv_all[own_rows, :] = own_dv[...].astype(BF16)
+    dv_gather.start()
     rk.take()
     lin = own_dk[...] * scale
     turned = lin * cos_scr[...] - pltpu.roll(lin, HD // 2, 1) * sin_scr[...]
     dk_all[own_rows, :] = turned.astype(BF16)
     dk_gather.start()
-    dv_gather.forward()
 
     def input_term(b):
         at = pl.ds(pl.multiple_of(b * width, width), width)
         return (dot_nt(dk_all[own_rows, :], wk_all[at, :])
                 + dot_nt(dv_all[own_rows, :], wv_all[at, :]))
-
-    cores = 2 if nf % 2 == 0 else 1
-    chips = nf // cores
-    chip = f // cores
-    core = f % cores
-    twin = chip * cores + (cores - 1 - core)
 
     def gi_twin(o):
         return copy(gi_send.at[o], gi_recv.at[o], gi_s.at[o], gi_r.at[o], (s, twin))
@@ -583,6 +775,14 @@
             twin_term(d)
         own_term(d)
         far_term(d)
+
+    if hosted:
+        pl.when(z == last)(lambda: last_relays("start", (wv_gather,)))
+
+        @pl.when(is_end(z))
+        def _():
+            for gather in (wk_gather, wv_gather):
+                gather.finish(last - z, last - z + 1)
 
     loop(1, chips, far_terms)
     if cores == 2:
@@ -600,6 +800,8 @@
                 grad = term if grad is None else grad + term
             out[...] = grad
 
+    pl.when(z >= outer // 2)(drain_early)
+    dv_gather.forward()
     dk_gather.forward()
     dv_gather.finish()
     if exchange:
@@ -619,13 +821,9 @@
     loop(1, chips, gi_take)
     gi_ref[...] = gi_own[chip].astype(BF16)
 
-    move_weights("wait_send")
-    relay_weights("wait_send")
-    for gather in (k_gather, v_gather, dk_gather, dv_gather):
+    for gather in (dk_gather, dv_gather):
         gather.drain()
     if exchange:
-        loop(0, s, lambda b: x_copy(b).wait_send())
-        loop(s + 1, n, lambda b: x_copy(b).wait_send())
         loop(1, nf, lambda d: xf_copy(d).wait_send())
     rv.drain()
     rk.drain()
@@ -685,8 +883,13 @@
         vmem((2 * nf, tok, width), BF16), vmem((2 * nf, tok, width), BF16),
         vmem((nf, tok, width), F32),
     ]
+    scratch += [vmem((tok, inner * rows), BF16)]
+    scratch += [vmem((2, tok, cols), BF16)] * 2
+    scratch += [pltpu.SemaphoreType.REGULAR((2,))]
+    scratch += [dma((2 * nf,)), dma((nf,)), dma((2,)), dma((2,))]
     scratch += [dma((hops,)), dma((pieces * n,))] * 2
-    scratch += [dma((2 * outer + 1,)), dma((n,))] * 4
+    scratch += [dma((2 * outer + 1,)), dma((n,))] * 2
+    scratch += [dma((1,)), dma((1,))] * 2 if exchange else [dma((2 * outer + 1,)), dma((n,))] * 2
     scratch += [dma((n,)), dma((n,)), dma((nf,)), dma((nf,))]
     scratch += [dma((n,)), dma((slots,))] * 2
     scratch += [dma((2 * nf,)), dma((2 * nf,))]

time: 66 us -> 63.2 us (0.958)
  Pallas kernels: 65.2 us -> 62.2 us
    pallas_call x1, Pallas kernels: 64.2 us -> 61.2 us  [body(): pl.pallas_call(functools.partial(kernel, (n, nf, exchange)), out_shape=[p...]
where the time goes in v3:
time: 63.2 us; the launch traced here: 62.9 us
  Pallas kernels  62.2 us (98%)
  between operations  0.64 us (1%)
    pallas_call x1, Pallas kernels, body(): pl.pallas_call(functools.partial(kernel, (n, nf, exchange)), out_shape=[p...  61.2 us

profile of v3, /device:TPU:0, one launch (start us, length us, event | category | flops | bytes accessed | tf_op | source)
XLA Modules:
  0.0 62.9 jit_solution(15445212007676013447)
XLA Ops:
  0.6 61.2 %shard_map.101 = (bf16[128,512]{1,0:T(8,128)(2,1)S(1)}, bf16[128,512]{1,0:T(8,128)(2,1)S(1)}, bf16[128,1024]{1,0:T(8,128)(2,1)S(1)}, f32[512,128]{1,0:T(8,128)S(1)}, f32[512,128]{1,0:T(8,128)S(1)}) custom-call(bf16[128,512]{1,0:T(8,128)(2,1)} %refs_0_.1, bf16[128,4096]{1,0:T(8,128)(2,1)} %refs_1_.1, bf16[512,128]{1,0:T(8,128)(2,1)} %refs_2_.1, ...), custom_call_target="tpu_custom_call" | custom-call | tf_op jit(solution)/shard_map/pallas_call | solution.py:907
  61.9 1.0 %shard_map.102 = (bf16[128,512]{1,0:T(8,128)(2,1)}, bf16[128,512]{1,0:T(8,128)(2,1)}, bf16[128,1024]{1,0:T(8,128)(2,1)}, f32[512,128]{1,0:T(8,128)}, f32[512,128]{1,0:T(8,128)}) custom-call(bf16[128,512]{1,0:T(8,128)(2,1)S(1)} %get-tuple-element.10.refs_0_, bf16[128,512]{1,0:T(8,128)(2,1)S(1)} %get-tuple-element.11.refs_1_, ...), custom_call_target="tpu_custom_call" | custom-call | tf_op jit(solution)/shard_map/pallas_call | solution.py:916

commit v4 on v3

--- a/solution.py
+++ b/solution.py
@@ -728,7 +728,15 @@
 
     if hosted:
         pl.when(z > outer // 2)(lambda: pl.semaphore_wait(told.at[0], 1))
-        pl.when(jnp.logical_and(z >= outer // 2, z < last))(lambda: tell(0, s + inner))
+
+        @pl.when(jnp.logical_and(z >= outer // 2, z < last))
+        def _():
+            if cores == 2:
+                pl.semaphore_signal(
+                    told.at[1], inc=1, device_id=(s, twin), device_id_type=MESH)
+                pl.semaphore_wait(told.at[1], 1)
+            tell(0, s + inner)
+
     rv.take()
     dv_all[own_rows, :] = own_dv[...].astype(BF16)
     dv_gather.start()

time: 63.2 us -> 62.3 us (0.986)
  Pallas kernels: 62.2 us -> 61.5 us
    pallas_call x1, Pallas kernels: 61.2 us -> 60.5 us  [body(): pl.pallas_call(functools.partial(kernel, (n, nf, exchange)), out_shape=[p...]
where the time goes in v4:
time: 62.3 us; the launch traced here: 62.1 us
  Pallas kernels  61.5 us (99%)
  between operations  0.64 us (1%)
    pallas_call x1, Pallas kernels, body(): pl.pallas_call(functools.partial(kernel, (n, nf, exchange)), out_shape=[p...  60.5 us

profile of v4, /device:TPU:0, one launch (start us, length us, event | category | flops | bytes accessed | tf_op | source)
XLA Modules:
  0.0 62.1 jit_solution(16716788878095586479)
XLA Ops:
  0.6 60.5 %shard_map.101 = (bf16[128,512]{1,0:T(8,128)(2,1)S(1)}, bf16[128,512]{1,0:T(8,128)(2,1)S(1)}, bf16[128,1024]{1,0:T(8,128)(2,1)S(1)}, f32[512,128]{1,0:T(8,128)S(1)}, f32[512,128]{1,0:T(8,128)S(1)}) custom-call(bf16[128,512]{1,0:T(8,128)(2,1)} %refs_0_.1, bf16[128,4096]{1,0:T(8,128)(2,1)} %refs_1_.1, bf16[512,128]{1,0:T(8,128)(2,1)} %refs_2_.1, ...), custom_call_target="tpu_custom_call" | custom-call | tf_op jit(solution)/shard_map/pallas_call | solution.py:915
  61.1 1.0 %shard_map.102 = (bf16[128,512]{1,0:T(8,128)(2,1)}, bf16[128,512]{1,0:T(8,128)(2,1)}, bf16[128,1024]{1,0:T(8,128)(2,1)}, f32[512,128]{1,0:T(8,128)}, f32[512,128]{1,0:T(8,128)}) custom-call(bf16[128,512]{1,0:T(8,128)(2,1)S(1)} %get-tuple-element.10.refs_0_, bf16[128,512]{1,0:T(8,128)(2,1)S(1)} %get-tuple-element.11.refs_1_, ...), custom_call_target="tpu_custom_call" | custom-call | tf_op jit(solution)/shard_map/pallas_call | solution.py:924

commit v5 on v4

--- a/solution.py
+++ b/solution.py
@@ -158,14 +158,9 @@
                 if inner == 2:
                     run(outer, z, 1 - y)
 
-            if self.causal:
-                far()
-                loop(0, outer - 1, lambda i: near(outer - 1 - i))
-                to_mate()
-            else:
-                to_mate()
-                loop(1, outer, near)
-                far()
+            far()
+            loop(0, outer - 1, lambda i: near(outer - 1 - i))
+            to_mate()
 
         def start(self):
             self.sends("start")

time: 62.3 us -> 61.9 us (level)
  no operation moved by 1% of the time
where the time goes in v5:
time: 61.9 us; the launch traced here: 61.7 us
  Pallas kernels  61.1 us (99%)
  between operations  0.64 us (1%)
    pallas_call x1, Pallas kernels, body(): pl.pallas_call(functools.partial(kernel, (n, nf, exchange)), out_shape=[p...  60.1 us

profile of v5, /device:TPU:0, one launch (start us, length us, event | category | flops | bytes accessed | tf_op | source)
XLA Modules:
  0.0 61.7 jit_solution(13987303520017559636)
XLA Ops:
  0.6 60.1 %shard_map.101 = (bf16[128,512]{1,0:T(8,128)(2,1)S(1)}, bf16[128,512]{1,0:T(8,128)(2,1)S(1)}, bf16[128,1024]{1,0:T(8,128)(2,1)S(1)}, f32[512,128]{1,0:T(8,128)S(1)}, f32[512,128]{1,0:T(8,128)S(1)}) custom-call(bf16[128,512]{1,0:T(8,128)(2,1)} %refs_0_.1, bf16[128,4096]{1,0:T(8,128)(2,1)} %refs_1_.1, bf16[512,128]{1,0:T(8,128)(2,1)} %refs_2_.1, ...), custom_call_target="tpu_custom_call" | custom-call | tf_op jit(solution)/shard_map/pallas_call | solution.py:910
  60.7 1.0 %shard_map.102 = (bf16[128,512]{1,0:T(8,128)(2,1)}, bf16[128,512]{1,0:T(8,128)(2,1)}, bf16[128,1024]{1,0:T(8,128)(2,1)}, f32[512,128]{1,0:T(8,128)}, f32[512,128]{1,0:T(8,128)}) custom-call(bf16[128,512]{1,0:T(8,128)(2,1)S(1)} %get-tuple-element.10.refs_0_, bf16[128,512]{1,0:T(8,128)(2,1)S(1)} %get-tuple-element.11.refs_1_, ...), custom_call_target="tpu_custom_call" | custom-call | tf_op jit(solution)/shard_map/pallas_call | solution.py:919

commit v6 on v5

--- a/solution.py
+++ b/solution.py
@@ -803,9 +803,9 @@
                 grad = term if grad is None else grad + term
             out[...] = grad
 
-    pl.when(z >= outer // 2)(drain_early)
     dv_gather.forward()
     dk_gather.forward()
+    pl.when(z >= outer // 2)(drain_early)
     dv_gather.finish()
     if exchange:
         loop(1, nf, xf_arrived)

time: 61.9 us -> 61.9 us (level)
  no operation moved by 1% of the time
where the time goes in v6:
time: 61.9 us; the launch traced here: 61.7 us
  Pallas kernels  61.1 us (99%)
  between operations  0.64 us (1%)
    pallas_call x1, Pallas kernels, body(): pl.pallas_call(functools.partial(kernel, (n, nf, exchange)), out_shape=[p...  60.1 us

profile of v6, /device:TPU:0, one launch (start us, length us, event | category | flops | bytes accessed | tf_op | source)
XLA Modules:
  0.0 61.7 jit_solution(12100224399064073729)
XLA Ops:
  0.6 60.1 %shard_map.101 = (bf16[128,512]{1,0:T(8,128)(2,1)S(1)}, bf16[128,512]{1,0:T(8,128)(2,1)S(1)}, bf16[128,1024]{1,0:T(8,128)(2,1)S(1)}, f32[512,128]{1,0:T(8,128)S(1)}, f32[512,128]{1,0:T(8,128)S(1)}) custom-call(bf16[128,512]{1,0:T(8,128)(2,1)} %refs_0_.1, bf16[128,4096]{1,0:T(8,128)(2,1)} %refs_1_.1, bf16[512,128]{1,0:T(8,128)(2,1)} %refs_2_.1, ...), custom_call_target="tpu_custom_call" | custom-call | tf_op jit(solution)/shard_map/pallas_call | solution.py:910
  60.7 1.0 %shard_map.102 = (bf16[128,512]{1,0:T(8,128)(2,1)}, bf16[128,512]{1,0:T(8,128)(2,1)}, bf16[128,1024]{1,0:T(8,128)(2,1)}, f32[512,128]{1,0:T(8,128)}, f32[512,128]{1,0:T(8,128)}) custom-call(bf16[128,512]{1,0:T(8,128)(2,1)S(1)} %get-tuple-element.10.refs_0_, bf16[128,512]{1,0:T(8,128)(2,1)S(1)} %get-tuple-element.11.refs_1_, ...), custom_call_target="tpu_custom_call" | custom-call | tf_op jit(solution)/shard_map/pallas_call | solution.py:919
